TPU v7x, 32 devices: a whole 2x2x4 slice. The times are simulated.
32 devices in a mesh: dp: 8 (over y, x, core), tensor: 4 (over z).
Axes of the slice: x: 2, y: 2, z: 4, core: 2. Of those that a mesh axis runs over, the one named last changes fastest.
Arguments:
- tokens: bfloat16 [4096, 2304], P(('dp', 'tensor')), may hold values from -6 to 6
- cotangent: bfloat16 [4096, 4096], P('dp', 'tensor'), may hold values from -6 to 6
- pre_gain: float32 [2304], replicated, may hold values from 0.25 to 1.75
- w_query: bfloat16 [2304, 4096], P('dp', 'tensor'), may hold values from -0.375 to 0.375
- key_weight: bfloat16 [2304, 2048], P('dp', 'tensor'), may hold values from -0.375 to 0.375
- value_weight: bfloat16 [2304, 2048], P('dp', 'tensor'), may hold values from -0.125 to 0.125
Outputs:
- attended: bfloat16 [4096, 4096], P('dp', 'tensor')
- grad_tokens: bfloat16 [4096, 2304], P(('dp', 'tensor'))
- grad_query: float32 [2304, 4096], P('dp', 'tensor')
- grad_key: float32 [2304, 2048], P('dp', 'tensor')
- grad_value: float32 [2304, 2048], P('dp', 'tensor')
- grad_pre_gain: float32 [2304], replicated
All inputs are finite; a program needn't handle non-finite values.
Results may differ from a plain program's by a relative error of at most 0.019.
The roundings to bfloat16 on the way count: a program that leaves them out, or rounds other values in their place, can miss the bound.
Values may be sent and summed in bfloat16 or wider, within the bound.
A program may use at most 192 MiB of HBM per device.

v0:
```python
import functools

import jax
import jax.numpy as jnp
import numpy as np
from jax import lax
from jax.experimental import pallas as pl
from jax.experimental.pallas import tpu as pltpu
from jax.sharding import PartitionSpec as P

HEAD_SIZE = 128
SEQ_LEN = 64


EPS = 1e-06
CAP = 50.0
BASE = 10000.0
query_scalar = 144.0


def rotary_tables(segment_length, half):
    places = jnp.arange(segment_length, dtype=jnp.float32)[:, None]
    freqs = BASE ** (-jnp.arange(half, dtype=jnp.float32) / half)
    angles = places * freqs[None, :]
    return (jnp.cos(angles)[:, None, :], jnp.sin(angles)[:, None, :])


def rotate(values, cosine_table, sine_table):
    half = values.shape[-1] // 2
    first, second = (values[..., :half], values[..., half:])
    return jnp.concatenate(
        [first * cosine_table - second * sine_table, second * cosine_table + first * sine_table], -1
    )


def inverse_rotation(values, cosine_table, sine_table):
    half = values.shape[-1] // 2
    first, second = (values[..., :half], values[..., half:])
    return jnp.concatenate(
        [first * cosine_table + second * sine_table, second * cosine_table - first * sine_table], -1
    )


def attend_forward(query, key, value):
    repeat = query.shape[1] // key.shape[1]
    keys = jnp.repeat(key, repeat, axis=1)
    values = jnp.repeat(value, repeat, axis=1)
    factor = query_scalar ** (-0.5)
    raw = jnp.einsum("qhd,khd->hqk", query, keys, preferred_element_type=jnp.float32) * factor
    bent = jnp.tanh(raw / CAP)
    capped = CAP * bent
    segment_length = query.shape[0]
    causal = jnp.arange(segment_length)[None, :] <= jnp.arange(segment_length)[:, None]
    raised = jnp.where(causal[None], jnp.exp(capped), 0.0)
    weights = raised / jnp.sum(raised, -1, keepdims=True)
    probs = weights.astype(jnp.bfloat16)
    attended = jnp.einsum("hqk,khd->qhd", probs, values, preferred_element_type=jnp.float32).astype(
        jnp.bfloat16
    )
    return (attended, weights, probs, bent)


def attend_backward(d_attended, query, key, value, weights, probs, bent):
    repeat = query.shape[1] // key.shape[1]
    keys = jnp.repeat(key, repeat, axis=1)
    values = jnp.repeat(value, repeat, axis=1)
    factor = query_scalar ** (-0.5)
    d_probs = jnp.einsum("qhd,khd->hqk", d_attended, values, preferred_element_type=jnp.float32)
    d_capped = weights * (d_probs - jnp.sum(weights * d_probs, -1, keepdims=True))
    d_scores = (d_capped * (1.0 - bent * bent) * factor).astype(jnp.bfloat16)
    query_back = jnp.einsum("hqk,khd->qhd", d_scores, keys, preferred_element_type=jnp.float32)
    key_heads = jnp.einsum("hqk,qhd->khd", d_scores, query, preferred_element_type=jnp.float32)
    value_heads = jnp.einsum("hqk,qhd->khd", probs, d_attended, preferred_element_type=jnp.float32)
    segment_length, heads, width = query.shape
    key_rotated_back = key_heads.reshape(segment_length, heads // repeat, repeat, width).sum(2)
    value_returned = value_heads.reshape(segment_length, heads // repeat, repeat, width).sum(2)
    return (query_back, key_rotated_back, value_returned)


def segment_pass(query, key, value, d_attended):
    attended, weights, probs, bent = attend_forward(query, key, value)
    query_back, key_rotated_back, value_returned = attend_backward(
        d_attended, query, key, value, weights, probs, bent
    )
    return (attended, query_back, key_rotated_back, value_returned)


def per_device(tokens, cotangent, pre_gain, w_query, key_weight, value_weight):
    contract_first = (((0,), (0,)), ((), ()))
    contract_last = (((1,), (1,)), ((), ()))
    rows_f = tokens.astype(jnp.float32)
    inv_one = lax.rsqrt(jnp.mean(rows_f * rows_f, -1, keepdims=True) + EPS)
    unit_one = rows_f * inv_one
    normed_input = (unit_one * pre_gain).astype(jnp.bfloat16)
    gathered = lax.all_gather(normed_input, "tensor", axis=0, tiled=True)
    segment_length = gathered.shape[0]
    token_span = SEQ_LEN
    pieces_count = segment_length // token_span
    heads_query = w_query.shape[1] // HEAD_SIZE
    heads_key = key_weight.shape[1] // HEAD_SIZE
    pieces = (
        lax.all_gather(w_query, "dp", axis=0, tiled=True),
        lax.all_gather(key_weight, "dp", axis=0, tiled=True),
        lax.all_gather(value_weight, "dp", axis=0, tiled=True),
    )
    query_raw, key_unrotated, value_projected = tuple(
        (jnp.dot(gathered, piece, preferred_element_type=jnp.float32) for piece in pieces)
    )
    cosine_table, sine_table = rotary_tables(token_span, HEAD_SIZE // 2)
    query = rotate(
        query_raw.reshape(pieces_count, token_span, heads_query, HEAD_SIZE),
        cosine_table,
        sine_table,
    ).astype(jnp.bfloat16)
    key = rotate(
        key_unrotated.reshape(pieces_count, token_span, heads_key, HEAD_SIZE),
        cosine_table,
        sine_table,
    ).astype(jnp.bfloat16)
    value = value_projected.reshape(pieces_count, token_span, heads_key, HEAD_SIZE).astype(
        jnp.bfloat16
    )
    d_attended = cotangent.reshape(pieces_count, token_span, heads_query, HEAD_SIZE)
    attended, query_back, key_rotated_back, value_returned = jax.vmap(segment_pass)(
        query, key, value, d_attended
    )
    attended_flat = attended.reshape(segment_length, heads_query * HEAD_SIZE)
    d_query = (
        inverse_rotation(query_back, cosine_table, sine_table)
        .astype(jnp.bfloat16)
        .reshape(segment_length, heads_query * HEAD_SIZE)
    )
    key_gradient = (
        inverse_rotation(key_rotated_back, cosine_table, sine_table)
        .astype(jnp.bfloat16)
        .reshape(segment_length, heads_key * HEAD_SIZE)
    )
    value_gradient = value_returned.astype(jnp.bfloat16).reshape(
        segment_length, heads_key * HEAD_SIZE
    )
    back_query, back_key, back_value = (
        lax.all_gather(w_query, "dp", axis=0, tiled=True),
        lax.all_gather(key_weight, "dp", axis=0, tiled=True),
        lax.all_gather(value_weight, "dp", axis=0, tiled=True),
    )
    joined = jnp.concatenate([d_query, key_gradient, value_gradient], 1)
    block = gathered
    grads = lax.psum_scatter(
        lax.dot_general(block, joined, contract_first, preferred_element_type=jnp.float32).astype(
            jnp.bfloat16
        ),
        "dp",
        scatter_dimension=0,
        tiled=True,
    ).astype(jnp.float32)
    width_query = w_query.shape[1]
    width_key = key_weight.shape[1]
    grad_query = grads[:, :width_query]
    grad_key = grads[:, width_query : width_query + width_key]
    grad_value = grads[:, width_query + width_key :]
    total = jnp.zeros((tokens.shape[0] * lax.axis_size("tensor"), gathered.shape[1]), jnp.float32)
    for grad_part, weight in (
        (d_query, back_query),
        (key_gradient, back_key),
        (value_gradient, back_value),
    ):
        block = grad_part
        total = total + lax.dot_general(
            block, weight, contract_last, preferred_element_type=jnp.float32
        )
    d_normed = lax.psum_scatter(
        total.astype(jnp.bfloat16), "tensor", scatter_dimension=0, tiled=True
    ).astype(jnp.float32)
    pre_part = jnp.sum(d_normed * unit_one, 0)
    scaled_in = d_normed * pre_gain
    grad_tokens = (
        inv_one * (scaled_in - unit_one * jnp.mean(scaled_in * unit_one, -1, keepdims=True))
    ).astype(jnp.bfloat16)
    grad_pre = lax.psum(pre_part, ("dp", "tensor"))
    return (attended_flat, grad_tokens, grad_query, grad_key, grad_value, grad_pre)


F32 = jnp.float32
BF16 = jnp.bfloat16
NN = (((1,), (0,)), ((), ()))
NT = (((1,), (1,)), ((), ()))
TN = (((0,), (0,)), ((), ()))


def swap_halves(values):
    half = values.shape[-1] // 2
    return jnp.concatenate([values[:, half:], values[:, :half]], -1)


def whole_kernel(
    dims,
    tok_ref,
    gain_ref,
    wq_ref,
    wk_ref,
    wv_ref,
    cot_ref,
    cos_ref,
    sin_ref,
    mask_ref,
    att_ref,
    gtok_ref,
    gq_ref,
    gk_ref,
    gv_ref,
    gpre_ref,
    x,
    xt,
    w,
    proj,
    dproj,
    g,
    pr,
    cs,
    dr,
    ar,
    dn,
    rb,
    pb1,
    pb2,
    ws,
    wr,
    xs,
    xr,
    gs,
    gr,
    zs,
    zr,
    ps,
    prs,
    ls,
):
    n_dp, n_t, chunks, rep, hd = dims
    dp = lax.axis_index("dp")
    t = lax.axis_index("tensor")
    rows = tok_ref.shape[0]
    width = tok_ref.shape[1]
    shard = wq_ref.shape[0]
    qw = rep * hd
    cw = qw + 2 * hd
    half = shard // 2
    core = lax.rem(dp, 2)
    chip = lax.div(dp, 2)
    mate, px, py = dp ^ 1, dp ^ 2, dp ^ 4

    def own_copies(j):
        here = pl.ds(pl.multiple_of(dp * shard, 16), shard)
        return (
            pltpu.make_async_copy(
                wq_ref.at[:, j * qw : (j + 1) * qw], w.at[j, here, 0:qw], ls.at[0, j]
            ),
            pltpu.make_async_copy(
                wk_ref.at[:, j * hd : (j + 1) * hd], w.at[j, here, qw : qw + hd], ls.at[1, j]
            ),
            pltpu.make_async_copy(
                wv_ref.at[:, j * hd : (j + 1) * hd], w.at[j, here, qw + hd : cw], ls.at[2, j]
            ),
        )

    for j in range(chunks):
        for copy in own_copies(j):
            copy.start()

    barrier = pltpu.get_barrier_semaphore()
    for o in range(1, n_dp):
        pl.semaphore_signal(
            barrier, inc=1, device_id=(dp ^ o, t), device_id_type=pl.DeviceIdType.MESH
        )
    for o in range(1, n_t):
        pl.semaphore_signal(
            barrier, inc=1, device_id=(dp, t ^ o), device_id_type=pl.DeviceIdType.MESH
        )
    pl.semaphore_wait(barrier, n_dp + n_t - 2)

    def rdma(src, dst, ssem, rsem, d, z):
        return pltpu.make_async_remote_copy(
            src_ref=src,
            dst_ref=dst,
            send_sem=ssem,
            recv_sem=rsem,
            device_id=(d, z),
            device_id_type=pl.DeviceIdType.MESH,
        )

    def wrow(who, h=None):
        if h is None:
            return pl.ds(pl.multiple_of(who * shard, 16), shard)
        return pl.ds(pl.multiple_of(who * shard + h * half, 16), half)

    def wcopy(kind, j, origin, to, h=None):
        place = w.at[j, wrow(origin, h)]
        return rdma(place, place, ws.at[kind, j], wr.at[kind, j], to, t)

    def offer(j):
        wcopy(0, j, dp, px).start()
        wcopy(1, j, dp, py).start()

    for j in range(chunks):
        for copy in own_copies(j):
            copy.wait()
        if j < 2:
            offer(j)

    tokens = tok_ref[...].astype(F32)
    inv = lax.rsqrt(jnp.mean(tokens * tokens, -1, keepdims=True) + EPS)
    x[pl.ds(pl.multiple_of(t * rows, rows), rows), :] = (
        (tokens * inv) * gain_ref[...][None, :]
    ).astype(BF16)

    piece = rows // 2

    def xcopy(way, o, h, origin, to):
        place = x.at[pl.ds(pl.multiple_of(origin * rows + h * piece, piece), piece)]
        return rdma(place, place, xs.at[way, o, h], xr.at[way, o, h], dp, to)

    @pl.when(t < n_t - 1)
    def _():
        for h in range(2):
            xcopy(0, 0, h, t, t + 1).start()

    @pl.when(t > 0)
    def _():
        for h in range(2):
            xcopy(1, 0, h, t, t - 1).start()

    for j in range(chunks):
        wcopy(2, j, dp, mate).start()

    def relay(j):
        wcopy(0, j, px, px).wait_recv()
        wcopy(5, j, px, py, h=0).start()
        wcopy(3, j, px, mate).start()
        wcopy(1, j, py, py).wait_recv()
        wcopy(6, j, py, px, h=1).start()
        wcopy(4, j, py, mate).start()

    def xrelay(o, h):
        @pl.when(t - o >= 0)
        def _():
            xcopy(0, o - 1, h, t - o, t).wait_recv()

            @pl.when(t + 1 < n_t)
            def _():
                xcopy(0, o, h, t - o, t + 1).start()

        @pl.when(t + o < n_t)
        def _():
            xcopy(1, o - 1, h, t + o, t).wait_recv()

            @pl.when(t > 0)
            def _():
                xcopy(1, o, h, t + o, t - 1).start()

    def far(j):
        wcopy(5, j, dp ^ 6, py, h=0).wait_recv()
        wcopy(6, j, dp ^ 6, px, h=1).wait_recv()
        wcopy(7, j, dp ^ 6, mate).start()

    def ready(j):
        far(j)
        wcopy(2, j, mate, mate).wait_recv()
        wcopy(3, j, dp ^ 3, mate).wait_recv()
        wcopy(4, j, dp ^ 5, mate).wait_recv()
        wcopy(7, j, dp ^ 7, mate).wait_recv()

    factor = query_scalar ** (-0.5)
    low = t < n_t // 2
    sign = jnp.where(low, 1, -1)
    m = jnp.where(low, t, n_t - 1 - t)
    fwd = jnp.where(low, 0, 1)

    def mirror(b):
        return jnp.where(low, b, n_t - 1 - b)

    places = (
        t,
        jnp.where(m == 0, t + sign, t - sign),
        jnp.where(m == 0, t + 2 * sign, t + sign),
        mirror(n_t - 1),
    )

    def head_cols(j, i):
        return pl.ds(pl.multiple_of(j * qw + i * hd, hd), hd)

    def tiles(*which):
        for slot, (j, p) in enumerate(which):
            here = pl.ds(pl.multiple_of(places[p] * rows, rows), rows)
            proj[slot] = lax.dot_general(x[here, :], w[j], NN, preferred_element_type=F32)
        for slot, (j, p) in enumerate(which):
            here = pl.ds(pl.multiple_of(places[p] * rows, rows), rows)
            cosv, sinv = cos_ref[...], sin_ref[...]

            def turn(v):
                return v * cosv + swap_halves(v) * sinv

            def unturn(v):
                return v * cosv - swap_halves(v) * sinv

            q = jnp.concatenate(
                [turn(proj[slot, :, i * hd : (i + 1) * hd]).astype(BF16) for i in range(rep)], 0
            )
            k = turn(proj[slot, :, qw : qw + hd]).astype(BF16)
            v = proj[slot, :, qw + hd : cw].astype(BF16)
            cot = jnp.concatenate(
                [cot_ref[here, head_cols(j, i)] for i in range(rep)], 0
            )
            bent = jnp.tanh(
                lax.dot_general(q, k, NT, preferred_element_type=F32) * factor / CAP
            )
            raised = jnp.exp(CAP * bent) * mask_ref[...]
            weights = raised / jnp.sum(raised, -1, keepdims=True)
            probs = weights.astype(BF16)
            att = lax.dot_general(probs, v, NN, preferred_element_type=F32).astype(BF16)
            d_probs = lax.dot_general(cot, v, NT, preferred_element_type=F32)
            d_capped = weights * (d_probs - jnp.sum(weights * d_probs, -1, keepdims=True))
            ds = (d_capped * (1.0 - bent * bent) * factor).astype(BF16)
            dq = lax.dot_general(ds, k, NN, preferred_element_type=F32)
            dk = lax.dot_general(ds, q, TN, preferred_element_type=F32)
            dv = lax.dot_general(probs, cot, TN, preferred_element_type=F32)
            for i in range(rep):
                part = slice(i * rows, (i + 1) * rows)
                att_ref[here, head_cols(j, i)] = att[part]
                dproj[j, here, i * hd : (i + 1) * hd] = unturn(dq[part]).astype(BF16)
            dproj[j, here, qw : qw + hd] = unturn(dk).astype(BF16)
            dproj[j, here, qw + hd : cw] = dv.astype(BF16)
    def zcopy(way, b, h, to):
        src = dn.at[pl.ds(pl.multiple_of(b * rows + h * piece, piece), piece)]
        return rdma(
            src,
            rb.at[way, b, pl.ds(h * piece, piece)],
            zs.at[way, b, h],
            zr.at[way, b, h],
            dp,
            to,
        )

    tile = 256

    def back(first, count):
        here = pl.ds(pl.multiple_of(first * rows, rows), count * rows)

        def cols(n, c2):
            span = pl.ds(pl.multiple_of(n * tile, tile), tile)
            total = lax.dot_general(
                dproj[0, here, :], w[0, span, :], NT, preferred_element_type=F32
            )
            for j in range(1, chunks):
                total += lax.dot_general(
                    dproj[j, here, :], w[j, span, :], NT, preferred_element_type=F32
                )
            dn[here, span] = total.astype(BF16)
            return c2

        lax.fori_loop(0, width // tile, cols, 0)

    def outward(b, halves=(0, 1)):
        for h in halves:
            zcopy(fwd, mirror(b), h, t + sign).start()

    def gcopy(kind, j, src, dst, to):
        return rdma(src, dst, gs.at[kind, j], gr.at[kind, j], to, t)

    def to_mate(j):
        return gcopy(0, j, g.at[j, :, 1 - core], pr.at[j], mate)

    lo, hi = pl.ds(0, half), pl.ds(half, half)
    cx, cy, cd = chip ^ 1, chip ^ 2, chip ^ 3

    def d_x(j):
        return gcopy(1, j, cs.at[j, cd, lo], dr.at[j, lo], px)

    def d_y(j):
        return gcopy(2, j, cs.at[j, cd, hi], dr.at[j, hi], py)

    def x_lo(j):
        return gcopy(3, j, cs.at[j, cx, lo], ar.at[0, j, lo], px)

    def x_hi(j):
        return gcopy(4, j, cs.at[j, cx, hi], ar.at[0, j, hi], px)

    def y_lo(j):
        return gcopy(5, j, cs.at[j, cy, lo], ar.at[1, j, lo], py)

    def y_hi(j):
        return gcopy(6, j, cs.at[j, cy, hi], ar.at[1, j, hi], py)

    def add(*parts):
        total = parts[0].astype(F32)
        for part in parts[1:]:
            total = total + part.astype(F32)
        return total.astype(BF16)

    def product(j):
        def share(c, c2):
            for k in range(2):
                span = pl.ds(pl.multiple_of((2 * c + k) * shard, 16), shard)
                g[j, c, k] = lax.dot_general(
                    xt[span, :], dproj[j], NN, preferred_element_type=F32
                ).astype(BF16)
            return c2

        lax.fori_loop(0, n_dp // 2, share, 0)
        to_mate(j).start()

    def on_chip(j):
        to_mate(j).wait_recv()
        for c in range(n_dp // 2):
            cs[j, c] = add(g[j, c, core], pr[j, c])
        d_x(j).start()
        d_y(j).start()
        x_lo(j).start()
        y_hi(j).start()

    def pass_on(j):
        d_x(j).wait_recv()
        cs[j, cy, lo] = add(cs[j, cy, lo], dr[j, lo])
        y_lo(j).start()
        d_y(j).wait_recv()
        cs[j, cx, hi] = add(cs[j, cx, hi], dr[j, hi])
        x_hi(j).start()

    def zsum(way, b, h):
        here = pl.ds(pl.multiple_of(b * rows + h * piece, piece), piece)
        zcopy(way, b, h, t).wait_recv()
        dn[here, :] = add(dn[here, :], rb[way, b, h * piece : (h + 1) * piece])

    far_block = mirror(n_t - 1)
    rest = jnp.where(low, 0, 1)

    relay(0)
    offer(2)
    xrelay(1, 0)
    relay(1)
    offer(3)
    xrelay(1, 1)
    ready(0)
    tiles((0, 0), (0, 1))
    xrelay(2, 0)
    relay(2)
    ready(1)
    xrelay(2, 1)
    tiles((1, 0), (1, 1))
    tiles((0, 2), (1, 2))
    relay(3)
    ready(2)
    tiles((2, 0), (2, 1), (2, 2))
    ready(3)
    xrelay(3, 0)
    xrelay(3, 1)
    tiles((0, 3), (1, 3))
    xt[...] = x[...].T
    product(0)
    tiles((2, 3), (3, 3))
    back(far_block, 1)

    @pl.when(m == 0)
    def _():
        outward(n_t - 1)

    on_chip(0)
    product(1)
    tiles((3, 0), (3, 1), (3, 2))
    back(rest, n_t - 1)

    @pl.when(m == 0)
    def _():
        outward(n_t - 2)
        outward(1)

    on_chip(1)
    product(2)

    @pl.when(m > 0)
    def _():
        for h in range(2):
            zsum(fwd, far_block, h)
            outward(n_t - 1, (h,))

    product(3)
    on_chip(2)
    pass_on(0)
    on_chip(3)
    pass_on(1)

    @pl.when(m > 0)
    def _():
        b = mirror(0)
        for h in range(2):
            zsum(1 - fwd, b, h)
            zcopy(1 - fwd, b, h, t - sign).start()
            zsum(fwd, mirror(n_t - 2), h)
            outward(n_t - 2, (h,))

    pass_on(2)
    pass_on(3)

    mine = pl.ds(pl.multiple_of(t * rows, rows), rows)
    for h in range(2):
        zcopy(1 - fwd, t, h, t).wait_recv()

    @pl.when(m > 0)
    def _():
        for h in range(2):
            zcopy(fwd, t, h, t).wait_recv()

    @pl.when(m == 0)
    def _():
        rb[fwd, t] = jnp.zeros((rows, width), BF16)

    d_normed = dn[mine, :].astype(F32) + rb[0, t].astype(F32) + rb[1, t].astype(F32)
    tokens2 = tok_ref[...].astype(F32)
    inv2 = lax.rsqrt(jnp.mean(tokens2 * tokens2, -1, keepdims=True) + EPS)
    unit = tokens2 * inv2
    pb1[dp] = jnp.sum(d_normed * unit, 0, keepdims=True)

    def p1(o):
        return rdma(pb1.at[dp], pb1.at[dp], ps.at[0, o], prs.at[0, o], dp ^ o, t)

    def p2(o):
        return rdma(pb2.at[t], pb2.at[t], ps.at[1, o], prs.at[1, o], dp, t ^ o)

    def p1r(o):
        return rdma(pb1.at[dp ^ o], pb1.at[dp ^ o], ps.at[0, o], prs.at[0, o], dp ^ o, t)

    def p2r(o):
        return rdma(pb2.at[t ^ o], pb2.at[t ^ o], ps.at[1, o], prs.at[1, o], dp, t ^ o)

    for o in range(1, n_dp):
        p1(o).start()
    e = d_normed * gain_ref[...][None, :]
    gtok_ref[...] = (inv2 * (e - unit * jnp.mean(e * unit, -1, keepdims=True))).astype(BF16)
    for o in range(1, n_dp):
        p1r(o).wait_recv()
    total = pb1[0]
    for o in range(1, n_dp):
        total = total + pb1[o]
    pb2[t] = total
    for o in range(1, n_t):
        p2(o).start()

    for j in range(chunks):
        x_lo(j).wait_recv()
        y_hi(j).wait_recv()
        y_lo(j).wait_recv()
        x_hi(j).wait_recv()
        done = add(cs[j, chip], ar[0, j], ar[1, j])
        gq_ref[:, j * qw : (j + 1) * qw] = done[:, :qw]
        gk_ref[:, j * hd : (j + 1) * hd] = done[:, qw : qw + hd]
        gv_ref[:, j * hd : (j + 1) * hd] = done[:, qw + hd :]

    for o in range(1, n_t):
        p2r(o).wait_recv()
    total = pb2[0]
    for o in range(1, n_t):
        total = total + pb2[o]
    gpre_ref[...] = total[0]

    for j in range(chunks):
        wcopy(0, j, dp, px).wait_send()
        wcopy(1, j, dp, py).wait_send()
        wcopy(2, j, dp, mate).wait_send()
        wcopy(3, j, px, mate).wait_send()
        wcopy(4, j, py, mate).wait_send()
        wcopy(5, j, px, py, h=0).wait_send()
        wcopy(6, j, py, px, h=1).wait_send()
        wcopy(7, j, dp ^ 6, mate).wait_send()
        to_mate(j).wait_send()
        for copy in (d_x, d_y, x_lo, x_hi, y_lo, y_hi):
            copy(j).wait_send()
    for h in range(2):
        for o in range(n_t - 1):
            @pl.when((t - o >= 0) & (t + 1 < n_t))
            def _():
                xcopy(0, o, h, t - o, t + 1).wait_send()

            @pl.when((t + o < n_t) & (t > 0))
            def _():
                xcopy(1, o, h, t + o, t - 1).wait_send()

        for b in range(n_t - 1, 0, -1):
            @pl.when(m < b)
            def _():
                zcopy(fwd, mirror(b), h, t + sign).wait_send()

        @pl.when(m > 0)
        def _():
            zcopy(1 - fwd, mirror(0), h, t - sign).wait_send()

    for o in range(1, n_dp):
        p1(o).wait_send()
    for o in range(1, n_t):
        p2(o).wait_send()


def fused_per_device(tokens, cotangent, pre_gain, w_query, key_weight, value_weight):
    n_dp, n_t = lax.axis_size("dp"), lax.axis_size("tensor")
    rows, width = tokens.shape
    block = rows * n_t
    shard = w_query.shape[0]
    chunks = key_weight.shape[1] // HEAD_SIZE
    rep = w_query.shape[1] // key_weight.shape[1]
    qw = rep * HEAD_SIZE
    cw = qw + 2 * HEAD_SIZE
    half = HEAD_SIZE // 2
    place = np.arange(rows)
    freqs = BASE ** (-np.arange(half) / half)
    angles = (place % SEQ_LEN)[:, None] * freqs[None, :]
    cosine = np.concatenate([np.cos(angles)] * 2, -1).astype(np.float32)
    sine = np.concatenate([-np.sin(angles), np.sin(angles)], -1).astype(np.float32)
    mask = (place[None, :] <= place[:, None]) & (
        place[None, :] // SEQ_LEN == place[:, None] // SEQ_LEN
    )
    mask = np.tile(mask.astype(np.float32), (rep, 1))
    vmem = pl.BlockSpec(memory_space=pltpu.VMEM)
    hbm = pl.BlockSpec(memory_space=pl.ANY)
    dma = pltpu.SemaphoreType.DMA
    attended, grad_tokens, gq, gk, gv, grad_pre = pl.pallas_call(
        functools.partial(whole_kernel, (n_dp, n_t, chunks, rep, HEAD_SIZE)),
        out_shape=(
            jax.ShapeDtypeStruct((block, chunks * qw), BF16),
            jax.ShapeDtypeStruct((rows, width), BF16),
            jax.ShapeDtypeStruct((shard, chunks * qw), BF16),
            jax.ShapeDtypeStruct((shard, chunks * HEAD_SIZE), BF16),
            jax.ShapeDtypeStruct((shard, chunks * HEAD_SIZE), BF16),
            jax.ShapeDtypeStruct((width,), F32),
        ),
        in_specs=[vmem, vmem, hbm, hbm, hbm] + [vmem] * 4,
        out_specs=(vmem,) * 6,
        scratch_shapes=[
            pltpu.VMEM((block, width), BF16),
            pltpu.VMEM((width, block), BF16),
            pltpu.VMEM((chunks, width, cw), BF16),
            pltpu.VMEM((3, rows, cw), F32),
            pltpu.VMEM((chunks, block, cw), BF16),
            pltpu.VMEM((chunks, n_dp // 2, 2, shard, cw), BF16),
            pltpu.VMEM((chunks, n_dp // 2, shard, cw), BF16),
            pltpu.VMEM((chunks, n_dp // 2, shard, cw), BF16),
            pltpu.VMEM((chunks, shard, cw), BF16),
            pltpu.VMEM((2, chunks, shard, cw), BF16),
            pltpu.VMEM((block, width), BF16),
            pltpu.VMEM((2, n_t, rows, width), BF16),
            pltpu.VMEM((n_dp, 1, width), F32),
            pltpu.VMEM((n_t, 1, width), F32),
            dma((8, chunks)),
            dma((8, chunks)),
            dma((2, n_t, 2)),
            dma((2, n_t, 2)),
            dma((7, chunks)),
            dma((7, chunks)),
            dma((2, n_t, 2)),
            dma((2, n_t, 2)),
            dma((2, n_dp)),
            dma((2, n_dp)),
            dma((3, chunks)),
        ],
        compiler_params=pltpu.CompilerParams(
            collective_id=0, has_side_effects=True, vmem_limit_bytes=62 * 1024 * 1024
        ),
    )(tokens, pre_gain, w_query, key_weight, value_weight, cotangent, cosine, sine, mask)
    return (
        attended,
        grad_tokens,
        gq.astype(F32),
        gk.astype(F32),
        gv.astype(F32),
        grad_pre,
    )


def solution(mesh):
    fused = mesh.shape["dp"] == 8 and mesh.shape["tensor"] == 4
    placed = (
        P(("dp", "tensor"), None),
        P("dp", "tensor"),
        P(),
        P("dp", "tensor"),
        P("dp", "tensor"),
        P("dp", "tensor"),
    )
    return jax.shard_map(
        fused_per_device if fused else per_device,
        mesh=mesh,
        in_specs=placed,
        out_specs=(
            P("dp", "tensor"),
            P(("dp", "tensor"), None),
            P("dp", "tensor"),
            P("dp", "tensor"),
            P("dp", "tensor"),
            P(),
        ),
        check_vma=False,
    )
```

profile of v0, /device:TPU:0, one launch (start us, length us, event | category | flops | bytes accessed | tf_op | source)
XLA Modules:
  0.0 118.1 jit_solution(16745415017488691760)
XLA Ops:
  0.6 110.5 %shard_map.136 = (bf16[512,1024]{1,0:T(8,128)(2,1)}, bf16[128,2304]{1,0:T(8,128)(2,1)}, bf16[288,1024]{1,0:T(8,128)(2,1)}, bf16[288,512]{1,0:T(8,128)(2,1)}, bf16[288,512]{1,0:T(8,128)(2,1)}, /*index=5*/f32[2304]{0:T(1024)}) custom-call(bf16[128,2304]{1,0:T(8,128)(2,1)} %tok_ref.1, f32[2304]{0:T(1024)} %gain_ref.1, bf16[288,1024]{1,0:T(8,128)(2,1)} %wq_ref.1, ...), custom_call_target="tpu_custom_call" | custom-call | tf_op jit(solution)/shard_map/pallas_call | solution.py:722
  111.2 0.0 copy-start.3
  111.2 0.0 copy-start.2
  111.2 2.3 %convert_element_type.9 = f32[288,1024]{1,0:T(8,128)} convert(bf16[288,1024]{1,0:T(8,128)(2,1)} %get-tuple-element.14) | non-fusion elementwise | flops 294912 | bytes 1769472 | tf_op jit(solution)/shard_map/convert_element_type | solution.py:768
  113.5 0.0 copy-start
  113.5 0.0 copy-done.3
  113.5 0.9 convert_element_type.10
  114.4 0.0 copy-done.2
  114.4 0.9 convert_element_type.11
  115.3 0.0 copy-start.1
  115.3 0.0 copy-done
  115.3 0.0 copy-start.4
  115.3 1.0 copy.18
  116.2 0.5 copy-done.1
  116.7 0.8 copy.19
  117.5 0.0 copy-done.4
  117.5 0.6 copy.20
Async XLA Ops:
  111.2 2.3 %copy-start.3 = (bf16[288,512]{1,0:T(8,128)(2,1)S(1)}, bf16[288,512]{1,0:T(8,128)(2,1)}, u32[]{:S(2)}) copy-start(bf16[288,512]{1,0:T(8,128)(2,1)} %get-tuple-element.15) | copy-start | bytes 884740
  111.2 3.2 %copy-start.2 = (bf16[288,512]{1,0:T(8,128)(2,1)S(1)}, bf16[288,512]{1,0:T(8,128)(2,1)}, u32[]{:S(2)}) copy-start(bf16[288,512]{1,0:T(8,128)(2,1)} %get-tuple-element.16) | copy-start | bytes 884740
  113.5 1.8 %copy-start = (bf16[512,1024]{1,0:T(8,128)(2,1)S(1)}, bf16[512,1024]{1,0:T(8,128)(2,1)}, u32[]{:S(2)}) copy-start(bf16[512,1024]{1,0:T(8,128)(2,1)} %get-tuple-element.24) | copy-start | bytes 3145732
  115.3 1.4 %copy-start.1 = (bf16[128,2304]{1,0:T(8,128)(2,1)S(1)}, bf16[128,2304]{1,0:T(8,128)(2,1)}, u32[]{:S(2)}) copy-start(bf16[128,2304]{1,0:T(8,128)(2,1)} %get-tuple-element.25) | copy-start | bytes 1769476
  115.3 2.3 %copy-start.4 = (f32[2304]{0:T(1024)S(1)}, f32[2304]{0:T(1024)}, u32[]{:S(2)}) copy-start(f32[2304]{0:T(1024)} %get-tuple-element.29) | copy-start | bytes 27652
where the time goes:
time: 118 us
  Pallas kernels  111 us (94%)
  other arithmetic  4.04 us (3%)
  local copies, waits for them, and re-layouts  2.87 us (2%)
    pallas_call x1, Pallas kernels, fused_per_device(): pl.pallas_call(functools.partial(whole_kernel, (n_dp, n_t, chunks, rep, H...  111 us
    unnamed x13, local copies, waits for them, and re-layouts  2.87 us

commit v1 on v0

--- a/solution.py
+++ b/solution.py
@@ -194,29 +194,35 @@
 
 def whole_kernel(
     dims,
-    tok_ref,
-    gain_ref,
+    tok_hbm,
+    gain_hbm,
     wq_ref,
     wk_ref,
     wv_ref,
-    cot_ref,
-    cos_ref,
-    sin_ref,
-    mask_ref,
+    cot_hbm,
+    cos_hbm,
+    sin_hbm,
+    mask_hbm,
     att_ref,
     gtok_ref,
     gq_ref,
     gk_ref,
     gv_ref,
     gpre_ref,
+    tok_ref,
+    gain_ref,
+    cot_ref,
+    cos_ref,
+    sin_ref,
+    mask_ref,
     x,
     xt,
     w,
+    wt,
     proj,
     dproj,
     g,
     pr,
-    cs,
     dr,
     ar,
     dn,
@@ -227,6 +233,8 @@
     wr,
     xs,
     xr,
+    ms,
+    mr,
     gs,
     gr,
     zs,
@@ -234,8 +242,9 @@
     ps,
     prs,
     ls,
+    ins,
 ):
-    n_dp, n_t, chunks, rep, hd = dims
+    n_dp, n_t, chunks, rep, hd, tile = dims
     dp = lax.axis_index("dp")
     t = lax.axis_index("tensor")
     rows = tok_ref.shape[0]
@@ -244,9 +253,35 @@
     qw = rep * hd
     cw = qw + 2 * hd
     half = shard // 2
+    n_chip = n_dp // 2
+    parts = width // tile
     core = lax.rem(dp, 2)
     chip = lax.div(dp, 2)
     mate, px, py = dp ^ 1, dp ^ 2, dp ^ 4
+
+    barrier = pltpu.get_barrier_semaphore()
+    for o in range(1, n_dp):
+        pl.semaphore_signal(
+            barrier, inc=1, device_id=(dp ^ o, t), device_id_type=pl.DeviceIdType.MESH
+        )
+    for o in range(1, n_t):
+        pl.semaphore_signal(
+            barrier, inc=1, device_id=(dp, t ^ o), device_id_type=pl.DeviceIdType.MESH
+        )
+
+    loads = [
+        pltpu.make_async_copy(src, dst, ins.at[i])
+        for i, (src, dst) in enumerate(
+            (
+                (tok_hbm, tok_ref),
+                (gain_hbm, gain_ref),
+                (cos_hbm, cos_ref),
+                (sin_hbm, sin_ref),
+                (mask_hbm, mask_ref),
+                (cot_hbm, cot_ref),
+            )
+        )
+    ]
 
     def own_copies(j):
         here = pl.ds(pl.multiple_of(dp * shard, 16), shard)
@@ -262,20 +297,13 @@
             ),
         )
 
+    loads[0].start()
+    loads[1].start()
     for j in range(chunks):
         for copy in own_copies(j):
             copy.start()
-
-    barrier = pltpu.get_barrier_semaphore()
-    for o in range(1, n_dp):
-        pl.semaphore_signal(
-            barrier, inc=1, device_id=(dp ^ o, t), device_id_type=pl.DeviceIdType.MESH
-        )
-    for o in range(1, n_t):
-        pl.semaphore_signal(
-            barrier, inc=1, device_id=(dp, t ^ o), device_id_type=pl.DeviceIdType.MESH
-        )
-    pl.semaphore_wait(barrier, n_dp + n_t - 2)
+    for copy in loads[2:]:
+        copy.start()
 
     def rdma(src, dst, ssem, rsem, d, z):
         return pltpu.make_async_remote_copy(
@@ -300,12 +328,8 @@
         wcopy(0, j, dp, px).start()
         wcopy(1, j, dp, py).start()
 
-    for j in range(chunks):
-        for copy in own_copies(j):
-            copy.wait()
-        if j < 2:
-            offer(j)
-
+    loads[0].wait()
+    loads[1].wait()
     tokens = tok_ref[...].astype(F32)
     inv = lax.rsqrt(jnp.mean(tokens * tokens, -1, keepdims=True) + EPS)
     x[pl.ds(pl.multiple_of(t * rows, rows), rows), :] = (
@@ -318,6 +342,11 @@
         place = x.at[pl.ds(pl.multiple_of(origin * rows + h * piece, piece), piece)]
         return rdma(place, place, xs.at[way, o, h], xr.at[way, o, h], dp, to)
 
+    for copy in own_copies(0):
+        copy.wait()
+    pl.semaphore_wait(barrier, n_dp + n_t - 2)
+    offer(0)
+
     @pl.when(t < n_t - 1)
     def _():
         for h in range(2):
@@ -328,8 +357,15 @@
         for h in range(2):
             xcopy(1, 0, h, t, t - 1).start()
 
+    for j in range(1, chunks):
+        for copy in own_copies(j):
+            copy.wait()
+        if j < 2:
+            offer(j)
     for j in range(chunks):
         wcopy(2, j, dp, mate).start()
+    for copy in loads[2:]:
+        copy.wait()
 
     def relay(j):
         wcopy(0, j, px, px).wait_recv()
@@ -361,8 +397,9 @@
         wcopy(6, j, dp ^ 6, px, h=1).wait_recv()
         wcopy(7, j, dp ^ 6, mate).start()
 
-    def ready(j):
-        far(j)
+    def ready(j, relayed=False):
+        if not relayed:
+            far(j)
         wcopy(2, j, mate, mate).wait_recv()
         wcopy(3, j, dp ^ 3, mate).wait_recv()
         wcopy(4, j, dp ^ 5, mate).wait_recv()
@@ -387,12 +424,15 @@
     def head_cols(j, i):
         return pl.ds(pl.multiple_of(j * qw + i * hd, hd), hd)
 
+    def block_rows(b, count=1):
+        return pl.ds(pl.multiple_of(b * rows, rows), count * rows)
+
     def tiles(*which):
         for slot, (j, p) in enumerate(which):
-            here = pl.ds(pl.multiple_of(places[p] * rows, rows), rows)
+            here = block_rows(places[p])
             proj[slot] = lax.dot_general(x[here, :], w[j], NN, preferred_element_type=F32)
         for slot, (j, p) in enumerate(which):
-            here = pl.ds(pl.multiple_of(places[p] * rows, rows), rows)
+            here = block_rows(places[p])
             cosv, sinv = cos_ref[...], sin_ref[...]
 
             def turn(v):
@@ -428,113 +468,181 @@
                 dproj[j, here, i * hd : (i + 1) * hd] = unturn(dq[part]).astype(BF16)
             dproj[j, here, qw : qw + hd] = unturn(dk).astype(BF16)
             dproj[j, here, qw + hd : cw] = dv.astype(BF16)
-    def zcopy(way, b, h, to):
-        src = dn.at[pl.ds(pl.multiple_of(b * rows + h * piece, piece), piece)]
+
+    def flip_rows(p):
+        here = block_rows(places[p])
+        xt[:, here] = x[here, :].T
+
+    def flip_weights(j):
+        wt[j] = w[j].T
+
+    def span(p):
+        return pl.ds(pl.multiple_of(p * tile, tile), tile)
+
+    def zcopy(way, b, p, to):
         return rdma(
-            src,
-            rb.at[way, b, pl.ds(h * piece, piece)],
-            zs.at[way, b, h],
-            zr.at[way, b, h],
+            dn.at[block_rows(b), span(p)],
+            rb.at[way, b, :, span(p)],
+            zs.at[way, b, p],
+            zr.at[way, b, p],
             dp,
             to,
         )
 
-    tile = 256
-
-    def back(first, count):
-        here = pl.ds(pl.multiple_of(first * rows, rows), count * rows)
-
-        def cols(n, c2):
-            span = pl.ds(pl.multiple_of(n * tile, tile), tile)
+    def outward(b, p):
+        zcopy(fwd, mirror(b), p, t + sign).start()
+
+    def back(first, count, sent):
+        here = block_rows(first, count)
+
+        def cols(p, c2):
             total = lax.dot_general(
-                dproj[0, here, :], w[0, span, :], NT, preferred_element_type=F32
+                dproj[0, here, :], wt[0, :, span(p)], NN, preferred_element_type=F32
             )
             for j in range(1, chunks):
                 total += lax.dot_general(
-                    dproj[j, here, :], w[j, span, :], NT, preferred_element_type=F32
+                    dproj[j, here, :], wt[j, :, span(p)], NN, preferred_element_type=F32
                 )
-            dn[here, span] = total.astype(BF16)
+            dn[here, span(p)] = total.astype(BF16)
+
+            @pl.when(m == 0)
+            def _():
+                outward(sent, p)
+
             return c2
 
-        lax.fori_loop(0, width // tile, cols, 0)
-
-    def outward(b, halves=(0, 1)):
-        for h in halves:
-            zcopy(fwd, mirror(b), h, t + sign).start()
+        lax.fori_loop(0, parts, cols, 0)
+
+    strip = 64
+
+    def gain_part(first, count, fresh):
+        def cols(p, c2):
+            def step(r, acc):
+                here = pl.ds(pl.multiple_of(first * rows + r * strip, strip), strip)
+                both = dn[here, span(p)].astype(F32) * x[here, span(p)].astype(F32)
+                return acc + jnp.sum(both.reshape(strip // 8, 8, tile), 0)
+
+            acc = lax.fori_loop(0, count * rows // strip, step, jnp.zeros((8, tile), F32))
+            total = jnp.sum(acc, 0, keepdims=True)
+            if not fresh:
+                total = total + pb1[dp, :, span(p)]
+            pb1[dp, :, span(p)] = total
+            return c2
+
+        lax.fori_loop(0, parts, cols, 0)
+
+    lo, hi = pl.ds(0, half), pl.ds(half, half)
+
+    def to_mate(j, i):
+        return rdma(g.at[j, i, 0], pr.at[j, i], ms.at[j, i], mr.at[j, i], mate, t)
 
     def gcopy(kind, j, src, dst, to):
         return rdma(src, dst, gs.at[kind, j], gr.at[kind, j], to, t)
 
-    def to_mate(j):
-        return gcopy(0, j, g.at[j, :, 1 - core], pr.at[j], mate)
-
-    lo, hi = pl.ds(0, half), pl.ds(half, half)
-    cx, cy, cd = chip ^ 1, chip ^ 2, chip ^ 3
-
     def d_x(j):
-        return gcopy(1, j, cs.at[j, cd, lo], dr.at[j, lo], px)
+        return gcopy(0, j, pr.at[j, 0, lo], dr.at[j, lo], px)
 
     def d_y(j):
-        return gcopy(2, j, cs.at[j, cd, hi], dr.at[j, hi], py)
+        return gcopy(1, j, pr.at[j, 0, hi], dr.at[j, hi], py)
 
     def x_lo(j):
-        return gcopy(3, j, cs.at[j, cx, lo], ar.at[0, j, lo], px)
+        return gcopy(2, j, pr.at[j, 2, lo], ar.at[0, j, lo], px)
 
     def x_hi(j):
-        return gcopy(4, j, cs.at[j, cx, hi], ar.at[0, j, hi], px)
+        return gcopy(3, j, pr.at[j, 2, hi], ar.at[0, j, hi], px)
 
     def y_lo(j):
-        return gcopy(5, j, cs.at[j, cy, lo], ar.at[1, j, lo], py)
+        return gcopy(4, j, pr.at[j, 1, lo], ar.at[1, j, lo], py)
 
     def y_hi(j):
-        return gcopy(6, j, cs.at[j, cy, hi], ar.at[1, j, hi], py)
-
-    def add(*parts):
-        total = parts[0].astype(F32)
-        for part in parts[1:]:
-            total = total + part.astype(F32)
+        return gcopy(5, j, pr.at[j, 1, hi], ar.at[1, j, hi], py)
+
+    def add(*terms):
+        total = terms[0].astype(F32)
+        for term in terms[1:]:
+            total = total + term.astype(F32)
         return total.astype(BF16)
 
-    def product(j):
-        def share(c, c2):
-            for k in range(2):
-                span = pl.ds(pl.multiple_of((2 * c + k) * shard, 16), shard)
-                g[j, c, k] = lax.dot_general(
-                    xt[span, :], dproj[j], NN, preferred_element_type=F32
+    def product(j, first=0, last=n_chip):
+        def share(i, c2):
+            c = chip ^ (n_chip - 1 - i)
+            for k, who in enumerate((2 * c + 1 - core, 2 * c + core)):
+                here = pl.ds(pl.multiple_of(who * shard, 16), shard)
+                g[j, i, k] = lax.dot_general(
+                    xt[here, :], dproj[j], NN, preferred_element_type=F32
                 ).astype(BF16)
+                if k == 0:
+                    to_mate(j, i).start()
             return c2
 
-        lax.fori_loop(0, n_dp // 2, share, 0)
-        to_mate(j).start()
-
-    def on_chip(j):
-        to_mate(j).wait_recv()
-        for c in range(n_dp // 2):
-            cs[j, c] = add(g[j, c, core], pr[j, c])
+        lax.fori_loop(first, last, share, 0)
+
+    def joined(j, i):
+        to_mate(j, i).wait_recv()
+        pr[j, i] = add(g[j, i, 1], pr[j, i])
+
+    def on_chip_far(j):
+        joined(j, 0)
         d_x(j).start()
         d_y(j).start()
+
+    def on_chip_near(j):
+        joined(j, 1)
+        y_hi(j).start()
+        joined(j, 2)
         x_lo(j).start()
-        y_hi(j).start()
 
     def pass_on(j):
         d_x(j).wait_recv()
-        cs[j, cy, lo] = add(cs[j, cy, lo], dr[j, lo])
+        pr[j, 1, lo] = add(pr[j, 1, lo], dr[j, lo])
         y_lo(j).start()
         d_y(j).wait_recv()
-        cs[j, cx, hi] = add(cs[j, cx, hi], dr[j, hi])
+        pr[j, 2, hi] = add(pr[j, 2, hi], dr[j, hi])
         x_hi(j).start()
 
-    def zsum(way, b, h):
-        here = pl.ds(pl.multiple_of(b * rows + h * piece, piece), piece)
-        zcopy(way, b, h, t).wait_recv()
-        dn[here, :] = add(dn[here, :], rb[way, b, h * piece : (h + 1) * piece])
+    def zsum(way, b, p):
+        here = block_rows(b)
+        cols = slice(p * tile, (p + 1) * tile)
+        zcopy(way, b, p, t).wait_recv()
+        dn[here, cols] = add(dn[here, cols], rb[way, b, :, cols])
 
     far_block = mirror(n_t - 1)
     rest = jnp.where(low, 0, 1)
+
+    def pass_far(p):
+        @pl.when(m > 0)
+        def _():
+            zsum(fwd, far_block, p)
+            outward(n_t - 1, p)
+
+    def pass_inner(p):
+        @pl.when(m > 0)
+        def _():
+            zsum(1 - fwd, mirror(0), p)
+            zcopy(1 - fwd, mirror(0), p, t - sign).start()
+
+    def pass_next(p):
+        @pl.when(m > 0)
+        def _():
+            zsum(fwd, mirror(n_t - 2), p)
+            outward(n_t - 2, p)
+
+    def p1(o):
+        return rdma(pb1.at[dp], pb1.at[dp], ps.at[0, o], prs.at[0, o], dp ^ o, t)
+
+    def p2(o):
+        return rdma(pb2.at[t], pb2.at[t], ps.at[1, o], prs.at[1, o], dp, t ^ o)
+
+    def p1r(o):
+        return rdma(pb1.at[dp ^ o], pb1.at[dp ^ o], ps.at[0, o], prs.at[0, o], dp ^ o, t)
+
+    def p2r(o):
+        return rdma(pb2.at[t ^ o], pb2.at[t ^ o], ps.at[1, o], prs.at[1, o], dp, t ^ o)
 
     relay(0)
     offer(2)
     xrelay(1, 0)
+    flip_rows(0)
     relay(1)
     offer(3)
     xrelay(1, 1)
@@ -542,98 +650,63 @@
     tiles((0, 0), (0, 1))
     xrelay(2, 0)
     relay(2)
+    flip_rows(1)
+    flip_weights(0)
     ready(1)
     xrelay(2, 1)
     tiles((1, 0), (1, 1))
     tiles((0, 2), (1, 2))
+    flip_rows(2)
     relay(3)
+    flip_weights(1)
     ready(2)
-    tiles((2, 0), (2, 1), (2, 2))
-    ready(3)
+    flip_weights(2)
+    tiles((2, 0), (2, 1))
     xrelay(3, 0)
     xrelay(3, 1)
-    tiles((0, 3), (1, 3))
-    xt[...] = x[...].T
-    product(0)
-    tiles((2, 3), (3, 3))
-    back(far_block, 1)
+    tiles((0, 3))
+    flip_rows(3)
+    far(3)
+    product(0, 0, 1)
+    ready(3, True)
+    tiles((1, 3), (2, 3), (3, 3))
+    on_chip_far(0)
+    flip_weights(3)
+    back(far_block, 1, n_t - 1)
+    product(0, 1)
+    product(1)
+    on_chip_near(0)
+    pass_on(0)
+    on_chip_far(1)
+    on_chip_near(1)
+    tiles((2, 2), (3, 2))
+    tiles((3, 0), (3, 1))
+    back(rest, n_t - 1, n_t - 2)
 
     @pl.when(m == 0)
     def _():
-        outward(n_t - 1)
-
-    on_chip(0)
-    product(1)
-    tiles((3, 0), (3, 1), (3, 2))
-    back(rest, n_t - 1)
-
-    @pl.when(m == 0)
-    def _():
-        outward(n_t - 2)
-        outward(1)
-
-    on_chip(1)
-    product(2)
-
-    @pl.when(m > 0)
-    def _():
-        for h in range(2):
-            zsum(fwd, far_block, h)
-            outward(n_t - 1, (h,))
-
-    product(3)
-    on_chip(2)
-    pass_on(0)
-    on_chip(3)
-    pass_on(1)
-
-    @pl.when(m > 0)
-    def _():
-        b = mirror(0)
-        for h in range(2):
-            zsum(1 - fwd, b, h)
-            zcopy(1 - fwd, b, h, t - sign).start()
-            zsum(fwd, mirror(n_t - 2), h)
-            outward(n_t - 2, (h,))
-
-    pass_on(2)
-    pass_on(3)
-
-    mine = pl.ds(pl.multiple_of(t * rows, rows), rows)
-    for h in range(2):
-        zcopy(1 - fwd, t, h, t).wait_recv()
-
-    @pl.when(m > 0)
-    def _():
-        for h in range(2):
-            zcopy(fwd, t, h, t).wait_recv()
-
-    @pl.when(m == 0)
-    def _():
-        rb[fwd, t] = jnp.zeros((rows, width), BF16)
-
-    d_normed = dn[mine, :].astype(F32) + rb[0, t].astype(F32) + rb[1, t].astype(F32)
-    tokens2 = tok_ref[...].astype(F32)
-    inv2 = lax.rsqrt(jnp.mean(tokens2 * tokens2, -1, keepdims=True) + EPS)
-    unit = tokens2 * inv2
-    pb1[dp] = jnp.sum(d_normed * unit, 0, keepdims=True)
-
-    def p1(o):
-        return rdma(pb1.at[dp], pb1.at[dp], ps.at[0, o], prs.at[0, o], dp ^ o, t)
-
-    def p2(o):
-        return rdma(pb2.at[t], pb2.at[t], ps.at[1, o], prs.at[1, o], dp, t ^ o)
-
-    def p1r(o):
-        return rdma(pb1.at[dp ^ o], pb1.at[dp ^ o], ps.at[0, o], prs.at[0, o], dp ^ o, t)
-
-    def p2r(o):
-        return rdma(pb2.at[t ^ o], pb2.at[t ^ o], ps.at[1, o], prs.at[1, o], dp, t ^ o)
-
+        for p in range(parts):
+            outward(1, p)
+
+    gain_part(rest, n_t - 1, True)
+    gain_part(far_block, 1, False)
+    pb1[dp] = pb1[dp] / gain_ref[...][None, :]
     for o in range(1, n_dp):
         p1(o).start()
-    e = d_normed * gain_ref[...][None, :]
-    gtok_ref[...] = (inv2 * (e - unit * jnp.mean(e * unit, -1, keepdims=True))).astype(BF16)
+    pass_far(0)
+    product(2)
+    pass_far(1)
+    on_chip_far(2)
+    on_chip_near(2)
+    pass_far(2)
+    pass_on(1)
+    product(3)
+    pass_inner(0)
+    on_chip_far(3)
+    on_chip_near(3)
+    pass_inner(1)
+    pass_next(0)
+    pass_inner(2)
     for o in range(1, n_dp):
         p1r(o).wait_recv()
     total = pb1[0]
@@ -642,23 +715,52 @@
     pb2[t] = total
     for o in range(1, n_t):
         p2(o).start()
-
+    pass_on(2)
+    pass_next(1)
     for j in range(chunks):
-        x_lo(j).wait_recv()
-        y_hi(j).wait_recv()
-        y_lo(j).wait_recv()
-        x_hi(j).wait_recv()
-        done = add(cs[j, chip], ar[0, j], ar[1, j])
-        gq_ref[:, j * qw : (j + 1) * qw] = done[:, :qw]
-        gk_ref[:, j * hd : (j + 1) * hd] = done[:, qw : qw + hd]
-        gv_ref[:, j * hd : (j + 1) * hd] = done[:, qw + hd :]
-
+        joined(j, 3)
+    pass_next(2)
+    pass_on(3)
     for o in range(1, n_t):
         p2r(o).wait_recv()
     total = pb2[0]
     for o in range(1, n_t):
         total = total + pb2[o]
     gpre_ref[...] = total[0]
+
+    def final(j):
+        x_lo(j).wait_recv()
+        y_hi(j).wait_recv()
+        y_lo(j).wait_recv()
+        x_hi(j).wait_recv()
+        done = add(pr[j, 3], ar[0, j], ar[1, j])
+        gq_ref[:, j * qw : (j + 1) * qw] = done[:, :qw]
+        gk_ref[:, j * hd : (j + 1) * hd] = done[:, qw : qw + hd]
+        gv_ref[:, j * hd : (j + 1) * hd] = done[:, qw + hd :]
+
+    for j in range(chunks - 1):
+        final(j)
+
+    mine = block_rows(t)
+    for p in range(parts):
+        zcopy(1 - fwd, t, p, t).wait_recv()
+
+    @pl.when(m > 0)
+    def _():
+        for p in range(parts):
+            zcopy(fwd, t, p, t).wait_recv()
+
+    @pl.when(m == 0)
+    def _():
+        rb[fwd, t] = jnp.zeros((rows, width), BF16)
+
+    d_normed = dn[mine, :].astype(F32) + rb[0, t].astype(F32) + rb[1, t].astype(F32)
+    tokens2 = tok_ref[...].astype(F32)
+    inv2 = lax.rsqrt(jnp.mean(tokens2 * tokens2, -1, keepdims=True) + EPS)
+    unit = tokens2 * inv2
+    e = d_normed * gain_ref[...][None, :]
+    gtok_ref[...] = (inv2 * (e - unit * jnp.mean(e * unit, -1, keepdims=True))).astype(BF16)
+    final(chunks - 1)
 
     for j in range(chunks):
         wcopy(0, j, dp, px).wait_send()
@@ -669,7 +771,8 @@
         wcopy(5, j, px, py, h=0).wait_send()
         wcopy(6, j, py, px, h=1).wait_send()
         wcopy(7, j, dp ^ 6, mate).wait_send()
-        to_mate(j).wait_send()
+        for i in range(n_chip):
+            to_mate(j, i).wait_send()
         for copy in (d_x, d_y, x_lo, x_hi, y_lo, y_hi):
             copy(j).wait_send()
     for h in range(2):
@@ -682,19 +785,35 @@
             def _():
                 xcopy(1, o, h, t + o, t - 1).wait_send()
 
+    for p in range(parts):
         for b in range(n_t - 1, 0, -1):
             @pl.when(m < b)
             def _():
-                zcopy(fwd, mirror(b), h, t + sign).wait_send()
+                zcopy(fwd, mirror(b), p, t + sign).wait_send()
 
         @pl.when(m > 0)
         def _():
-            zcopy(1 - fwd, mirror(0), h, t - sign).wait_send()
+            zcopy(1 - fwd, mirror(0), p, t - sign).wait_send()
 
     for o in range(1, n_dp):
         p1(o).wait_send()
     for o in range(1, n_t):
         p2(o).wait_send()
+
+
+def finish_kernel(att, gtok, gq, gk, gv, gpre, *refs):
+    outs, (bq, bk, bv), sems = refs[:6], refs[6:9], refs[9]
+    copies = [
+        pltpu.make_async_copy(src, outs[i], sems.at[i])
+        for src, i in ((att, 0), (gtok, 1), (bq, 2), (bk, 3), (bv, 4), (gpre, 5))
+    ]
+    for i in (0, 1, 5):
+        copies[i].start()
+    for src, wide, i in ((gq, bq, 2), (gk, bk, 3), (gv, bv, 4)):
+        wide[...] = src[...].astype(F32)
+        copies[i].start()
+    for copy in copies:
+        copy.wait()
 
 
 def fused_per_device(tokens, cotangent, pre_gain, w_query, key_weight, value_weight):
@@ -706,7 +825,10 @@
     rep = w_query.shape[1] // key_weight.shape[1]
     qw = rep * HEAD_SIZE
     cw = qw + 2 * HEAD_SIZE
+    kw = chunks * HEAD_SIZE
     half = HEAD_SIZE // 2
+    parts = 3 if width % (3 * HEAD_SIZE) == 0 else 1
+    n_chip = n_dp // 2
     place = np.arange(rows)
     freqs = BASE ** (-np.arange(half) / half)
     angles = (place % SEQ_LEN)[:, None] * freqs[None, :]
@@ -719,27 +841,33 @@
     vmem = pl.BlockSpec(memory_space=pltpu.VMEM)
     hbm = pl.BlockSpec(memory_space=pl.ANY)
     dma = pltpu.SemaphoreType.DMA
-    attended, grad_tokens, gq, gk, gv, grad_pre = pl.pallas_call(
-        functools.partial(whole_kernel, (n_dp, n_t, chunks, rep, HEAD_SIZE)),
+    made = pl.pallas_call(
+        functools.partial(whole_kernel, (n_dp, n_t, chunks, rep, HEAD_SIZE, width // parts)),
         out_shape=(
-            jax.ShapeDtypeStruct((block, chunks * qw), BF16),
-            jax.ShapeDtypeStruct((rows, width), BF16),
-            jax.ShapeDtypeStruct((shard, chunks * qw), BF16),
-            jax.ShapeDtypeStruct((shard, chunks * HEAD_SIZE), BF16),
-            jax.ShapeDtypeStruct((shard, chunks * HEAD_SIZE), BF16),
-            jax.ShapeDtypeStruct((width,), F32),
+            pltpu.VMEM((block, chunks * qw), BF16),
+            pltpu.VMEM((rows, width), BF16),
+            pltpu.VMEM((shard, chunks * qw), BF16),
+            pltpu.VMEM((shard, kw), BF16),
+            pltpu.VMEM((shard, kw), BF16),
+            pltpu.VMEM((width,), F32),
         ),
-        in_specs=[vmem, vmem, hbm, hbm, hbm] + [vmem] * 4,
+        in_specs=[hbm] * 9,
         out_specs=(vmem,) * 6,
         scratch_shapes=[
+            pltpu.VMEM((rows, width), BF16),
+            pltpu.VMEM((width,), F32),
+            pltpu.VMEM((block, chunks * qw), BF16),
+            pltpu.VMEM(cosine.shape, F32),
+            pltpu.VMEM(sine.shape, F32),
+            pltpu.VMEM(mask.shape, F32),
             pltpu.VMEM((block, width), BF16),
             pltpu.VMEM((width, block), BF16),
             pltpu.VMEM((chunks, width, cw), BF16),
+            pltpu.VMEM((chunks, cw, width), BF16),
             pltpu.VMEM((3, rows, cw), F32),
             pltpu.VMEM((chunks, block, cw), BF16),
-            pltpu.VMEM((chunks, n_dp // 2, 2, shard, cw), BF16),
-            pltpu.VMEM((chunks, n_dp // 2, shard, cw), BF16),
-            pltpu.VMEM((chunks, n_dp // 2, shard, cw), BF16),
+            pltpu.VMEM((chunks, n_chip, 2, shard, cw), BF16),
+            pltpu.VMEM((chunks, n_chip, shard, cw), BF16),
             pltpu.VMEM((chunks, shard, cw), BF16),
             pltpu.VMEM((2, chunks, shard, cw), BF16),
             pltpu.VMEM((block, width), BF16),
@@ -750,26 +878,41 @@
             dma((8, chunks)),
             dma((2, n_t, 2)),
             dma((2, n_t, 2)),
-            dma((7, chunks)),
-            dma((7, chunks)),
-            dma((2, n_t, 2)),
-            dma((2, n_t, 2)),
+            dma((chunks, n_chip)),
+            dma((chunks, n_chip)),
+            dma((6, chunks)),
+            dma((6, chunks)),
+            dma((2, n_t, parts)),
+            dma((2, n_t, parts)),
             dma((2, n_dp)),
             dma((2, n_dp)),
             dma((3, chunks)),
+            dma((6,)),
         ],
         compiler_params=pltpu.CompilerParams(
-            collective_id=0, has_side_effects=True, vmem_limit_bytes=62 * 1024 * 1024
+            collective_id=0, has_side_effects=True, vmem_limit_bytes=58 * 1024 * 1024
         ),
     )(tokens, pre_gain, w_query, key_weight, value_weight, cotangent, cosine, sine, mask)
-    return (
-        attended,
-        grad_tokens,
-        gq.astype(F32),
-        gk.astype(F32),
-        gv.astype(F32),
-        grad_pre,
-    )
+    return pl.pallas_call(
+        finish_kernel,
+        out_shape=(
+            jax.ShapeDtypeStruct((block, chunks * qw), BF16),
+            jax.ShapeDtypeStruct((rows, width), BF16),
+            jax.ShapeDtypeStruct((shard, chunks * qw), F32),
+            jax.ShapeDtypeStruct((shard, kw), F32),
+            jax.ShapeDtypeStruct((shard, kw), F32),
+            jax.ShapeDtypeStruct((width,), F32),
+        ),
+        in_specs=[vmem] * 6,
+        out_specs=(hbm,) * 6,
+        scratch_shapes=[
+            pltpu.VMEM((shard, chunks * qw), F32),
+            pltpu.VMEM((shard, kw), F32),
+            pltpu.VMEM((shard, kw), F32),
+            dma((6,)),
+        ],
+        compiler_params=pltpu.CompilerParams(vmem_limit_bytes=16 * 1024 * 1024),
+    )(*made)
 
 
 def solution(mesh):

time: 118 us -> 102 us (0.86)
  Pallas kernels: 111 us -> 101 us
  other arithmetic: 4.04 us -> 0 us
  local copies, waits for them, and re-layouts: 2.87 us -> 0 us
    pallas_call x1, Pallas kernels: 111 us -> 98.7 us  [fused_per_device(): pl.pallas_call(functools.partial(whole_kernel, (n_dp, n_t, chunks, rep, H...]
    convert_element_type x3 -> x0, other arithmetic: 4.04 us -> none  [the longest x1 2.27 us: fused_per_device(): gq.astype(F32)]
    unnamed x13 -> x0, local copies, waits for them, and re-layouts: 2.87 us -> none
    pallas_call x0 -> x1, Pallas kernels: none -> 2 us  [fused_per_device(): pl.pallas_call(finish_kernel, out_shape=(jax.ShapeDtypeStruct((block, chu...]
where the time goes in v1:
time: 102 us
  Pallas kernels  101 us (99%)
    pallas_call x1, Pallas kernels, fused_per_device(): pl.pallas_call(functools.partial(whole_kernel, (n_dp, n_t, chunks, rep, H...  98.7 us

profile of v1, /device:TPU:0, one launch (start us, length us, event | category | flops | bytes accessed | tf_op | source)
XLA Modules:
  0.0 101.5 jit_solution(7084362200859270313)
XLA Ops:
  0.6 98.7 %shard_map.136 = (bf16[512,1024]{1,0:T(8,128)(2,1)S(1)}, bf16[128,2304]{1,0:T(8,128)(2,1)S(1)}, bf16[288,1024]{1,0:T(8,128)(2,1)S(1)}, bf16[288,512]{1,0:T(8,128...) custom-call(bf16[128,2304]{1,0:T(8,128)(2,1)} %tok_hbm.1, f32[2304]{0:T(1024)} %gain_hbm.1, ...), custom_call_target="tpu_custom_call" | custom-call | tf_op jit(solution)/shard_map/pallas_call | solution.py:844
  99.4 2.0 %shard_map.137 = (bf16[512,1024]{1,0:T(8,128)(2,1)}, bf16[128,2304]{1,0:T(8,128)(2,1)}, f32[288,1024]{1,0:T(8,128)}, f32[288,512]{1,0:T(8,128)}, f32[288,512]{1,0:T(8,128)}, /*index=5*/f32[2304]{0:T(1024)}) custom-call(bf16[512,1024]{1,0:T(8,128)(2,1)S(1)} %get-tuple-element.12.att, bf16[128,2304]{1,0:T(8,128)(2,1)S(1)} %get-tuple-element.13.gtok, ...), custom_call_target="tpu_custom_call" | custom-call | tf_op jit(solution)/shard_map/pallas_call | solution.py:896

commit v2 on v1

--- a/solution.py
+++ b/solution.py
@@ -233,6 +233,8 @@
     wr,
     xs,
     xr,
+    qs,
+    qr,
     ms,
     mr,
     gs,
@@ -260,14 +262,24 @@
     mate, px, py = dp ^ 1, dp ^ 2, dp ^ 4
 
     barrier = pltpu.get_barrier_semaphore()
-    for o in range(1, n_dp):
+
+    def greet(d, z):
         pl.semaphore_signal(
-            barrier, inc=1, device_id=(dp ^ o, t), device_id_type=pl.DeviceIdType.MESH
+            barrier, inc=1, device_id=(d, z), device_id_type=pl.DeviceIdType.MESH
         )
-    for o in range(1, n_t):
-        pl.semaphore_signal(
-            barrier, inc=1, device_id=(dp, t ^ o), device_id_type=pl.DeviceIdType.MESH
-        )
+
+    greet(px, t)
+    greet(py, t)
+
+    @pl.when(t < n_t - 1)
+    def _():
+        greet(dp, t + 1)
+
+    @pl.when(t > 0)
+    def _():
+        greet(dp, t - 1)
+
+    greet(mate, t)
 
     loads = [
         pltpu.make_async_copy(src, dst, ins.at[i])
@@ -328,6 +340,28 @@
         wcopy(0, j, dp, px).start()
         wcopy(1, j, dp, py).start()
 
+    low = t < n_t // 2
+    sign = jnp.where(low, 1, -1)
+    m = jnp.where(low, t, n_t - 1 - t)
+    fwd = jnp.where(low, 0, 1)
+    piece, quarter = rows // 2, rows // 4
+
+    def xcopy(way, o, h, origin, to):
+        place = x.at[pl.ds(pl.multiple_of(origin * rows + h * piece, piece), piece)]
+        return rdma(place, place, xs.at[way, o, h], xr.at[way, o, h], dp, to)
+
+    def qcopy(k, origin, to):
+        first = pl.multiple_of(origin * rows + piece + k * quarter, quarter)
+        place = x.at[pl.ds(first, quarter)]
+        return rdma(place, place, qs.at[k], qr.at[k], dp, to)
+
+    for copy in own_copies(0):
+        copy.wait()
+    pl.semaphore_wait(barrier, 3 + jnp.where(m == 0, 1, 2))
+    offer(0)
+    for copy in own_copies(1):
+        copy.wait()
+    offer(1)
     loads[0].wait()
     loads[1].wait()
     tokens = tok_ref[...].astype(F32)
@@ -336,32 +370,29 @@
         (tokens * inv) * gain_ref[...][None, :]
     ).astype(BF16)
 
-    piece = rows // 2
-
-    def xcopy(way, o, h, origin, to):
-        place = x.at[pl.ds(pl.multiple_of(origin * rows + h * piece, piece), piece)]
-        return rdma(place, place, xs.at[way, o, h], xr.at[way, o, h], dp, to)
-
-    for copy in own_copies(0):
-        copy.wait()
-    pl.semaphore_wait(barrier, n_dp + n_t - 2)
-    offer(0)
-
     @pl.when(t < n_t - 1)
     def _():
-        for h in range(2):
-            xcopy(0, 0, h, t, t + 1).start()
+        xcopy(0, 0, 0, t, t + 1).start()
 
     @pl.when(t > 0)
     def _():
-        for h in range(2):
-            xcopy(1, 0, h, t, t - 1).start()
-
-    for j in range(1, chunks):
+        xcopy(1, 0, 0, t, t - 1).start()
+
+    @pl.when(t < n_t - 2)
+    def _():
+        xcopy(0, 0, 1, t, t + 1).start()
+
+    @pl.when(t > 1)
+    def _():
+        xcopy(1, 0, 1, t, t - 1).start()
+
+    @pl.when(m > 0)
+    def _():
+        qcopy(0, t, t - sign).start()
+
+    for j in range(2, chunks):
         for copy in own_copies(j):
             copy.wait()
-        if j < 2:
-            offer(j)
     for j in range(chunks):
         wcopy(2, j, dp, mate).start()
     for copy in loads[2:]:
@@ -376,7 +407,11 @@
         wcopy(4, j, py, mate).start()
 
     def xrelay(o, h):
-        @pl.when(t - o >= 0)
+        split = o == 1 and h == 1
+        above = (t - o >= 0) & (t < n_t - 1) if split else t - o >= 0
+        below = (t + o < n_t) & (t > 0) if split else t + o < n_t
+
+        @pl.when(above)
         def _():
             xcopy(0, o - 1, h, t - o, t).wait_recv()
 
@@ -384,13 +419,24 @@
             def _():
                 xcopy(0, o, h, t - o, t + 1).start()
 
-        @pl.when(t + o < n_t)
+        @pl.when(below)
         def _():
             xcopy(1, o - 1, h, t + o, t).wait_recv()
 
             @pl.when(t > 0)
             def _():
                 xcopy(1, o, h, t + o, t - 1).start()
+
+    def xlate():
+        @pl.when(m > 0)
+        def _():
+            qcopy(1, t, t - sign).start()
+
+    def xfinish():
+        @pl.when(m == 0)
+        def _():
+            for k in range(2):
+                qcopy(k, t + sign, t).wait_recv()
 
     def far(j):
         wcopy(5, j, dp ^ 6, py, h=0).wait_recv()
@@ -406,10 +452,6 @@
         wcopy(7, j, dp ^ 7, mate).wait_recv()
 
     factor = query_scalar ** (-0.5)
-    low = t < n_t // 2
-    sign = jnp.where(low, 1, -1)
-    m = jnp.where(low, t, n_t - 1 - t)
-    fwd = jnp.where(low, 0, 1)
 
     def mirror(b):
         return jnp.where(low, b, n_t - 1 - b)
@@ -525,8 +567,8 @@
             acc = lax.fori_loop(0, count * rows // strip, step, jnp.zeros((8, tile), F32))
             total = jnp.sum(acc, 0, keepdims=True)
             if not fresh:
-                total = total + pb1[dp, :, span(p)]
-            pb1[dp, :, span(p)] = total
+                total = total + pb1[t, :, span(p)]
+            pb1[t, :, span(p)] = total
             return c2
 
         lax.fori_loop(0, parts, cols, 0)
@@ -628,16 +670,26 @@
             outward(n_t - 2, p)
 
     def p1(o):
-        return rdma(pb1.at[dp], pb1.at[dp], ps.at[0, o], prs.at[0, o], dp ^ o, t)
+        return rdma(pb1.at[t], pb1.at[t], ps.at[0, o], prs.at[0, o], dp, t ^ o)
 
     def p2(o):
-        return rdma(pb2.at[t], pb2.at[t], ps.at[1, o], prs.at[1, o], dp, t ^ o)
+        return rdma(pb2.at[dp], pb2.at[dp], ps.at[1, o], prs.at[1, o], dp ^ o, t)
 
     def p1r(o):
-        return rdma(pb1.at[dp ^ o], pb1.at[dp ^ o], ps.at[0, o], prs.at[0, o], dp ^ o, t)
+        return rdma(pb1.at[t ^ o], pb1.at[t ^ o], ps.at[0, o], prs.at[0, o], dp, t ^ o)
 
     def p2r(o):
-        return rdma(pb2.at[t ^ o], pb2.at[t ^ o], ps.at[1, o], prs.at[1, o], dp, t ^ o)
+        return rdma(pb2.at[dp ^ o], pb2.at[dp ^ o], ps.at[1, o], prs.at[1, o], dp ^ o, t)
+
+    def final(j):
+        x_lo(j).wait_recv()
+        y_hi(j).wait_recv()
+        y_lo(j).wait_recv()
+        x_hi(j).wait_recv()
+        done = pr[j, 3].astype(F32) + ar[0, j].astype(F32) + ar[1, j].astype(F32)
+        gq_ref[:, j * qw : (j + 1) * qw] = done[:, :qw]
+        gk_ref[:, j * hd : (j + 1) * hd] = done[:, qw : qw + hd]
+        gv_ref[:, j * hd : (j + 1) * hd] = done[:, qw + hd :]
 
     relay(0)
     offer(2)
@@ -647,121 +699,89 @@
     offer(3)
     xrelay(1, 1)
     ready(0)
-    tiles((0, 0), (0, 1))
+    tiles((0, 0))
     xrelay(2, 0)
     relay(2)
-    flip_rows(1)
     flip_weights(0)
     ready(1)
     xrelay(2, 1)
-    tiles((1, 0), (1, 1))
-    tiles((0, 2), (1, 2))
+    xlate()
+    tiles((1, 0), (0, 2), (1, 2))
     flip_rows(2)
     relay(3)
     flip_weights(1)
-    ready(2)
-    flip_weights(2)
-    tiles((2, 0), (2, 1))
+    far(2)
     xrelay(3, 0)
     xrelay(3, 1)
-    tiles((0, 3))
+    tiles((0, 3), (1, 3))
     flip_rows(3)
+    ready(2, True)
+    flip_weights(2)
     far(3)
+    tiles((2, 3))
+    xfinish()
+    tiles((0, 1))
+    flip_rows(1)
     product(0, 0, 1)
     ready(3, True)
-    tiles((1, 3), (2, 3), (3, 3))
+    tiles((3, 3))
     on_chip_far(0)
     flip_weights(3)
     back(far_block, 1, n_t - 1)
-    product(0, 1)
-    product(1)
+    gain_part(far_block, 1, True)
+    product(0, 1, 3)
     on_chip_near(0)
+    tiles((1, 1))
+    product(1, 0, 3)
     pass_on(0)
     on_chip_far(1)
+    tiles((2, 0), (2, 1), (2, 2))
     on_chip_near(1)
-    tiles((2, 2), (3, 2))
-    tiles((3, 0), (3, 1))
+    pass_far(0)
+    tiles((3, 0), (3, 1), (3, 2))
+    product(2, 0, 1)
     back(rest, n_t - 1, n_t - 2)
+    on_chip_far(2)
+    gain_part(rest, n_t - 1, False)
+    pb1[t] = pb1[t] / gain_ref[...][None, :]
+    for o in range(1, n_t):
+        p1(o).start()
 
     @pl.when(m == 0)
     def _():
         for p in range(parts):
             outward(1, p)
 
-    gain_part(rest, n_t - 1, True)
-    gain_part(far_block, 1, False)
-    pb1[dp] = pb1[dp] / gain_ref[...][None, :]
-    for o in range(1, n_dp):
-        p1(o).start()
-    pass_far(0)
-    product(2)
+    pass_on(1)
     pass_far(1)
-    on_chip_far(2)
+    pass_far(2)
+    product(2, 1, 3)
     on_chip_near(2)
-    pass_far(2)
-    pass_on(1)
-    product(3)
+    product(3, 0, 3)
     pass_inner(0)
     on_chip_far(3)
+    product(0, 3, 4)
+    product(1, 3, 4)
     on_chip_near(3)
     pass_inner(1)
     pass_next(0)
+    pass_on(2)
+    product(2, 3, 4)
+    product(3, 3, 4)
     pass_inner(2)
-    for o in range(1, n_dp):
+    pass_next(1)
+    for o in range(1, n_t):
         p1r(o).wait_recv()
     total = pb1[0]
+    for o in range(1, n_t):
+        total = total + pb1[o]
+    pb2[dp] = total
     for o in range(1, n_dp):
-        total = total + pb1[o]
-    pb2[t] = total
-    for o in range(1, n_t):
         p2(o).start()
-    pass_on(2)
-    pass_next(1)
+    pass_next(2)
     for j in range(chunks):
         joined(j, 3)
-    pass_next(2)
     pass_on(3)
-    for o in range(1, n_t):
-        p2r(o).wait_recv()
-    total = pb2[0]
-    for o in range(1, n_t):
-        total = total + pb2[o]
-    gpre_ref[...] = total[0]
-
-    def final(j):
-        x_lo(j).wait_recv()
-        y_hi(j).wait_recv()
-        y_lo(j).wait_recv()
-        x_hi(j).wait_recv()
-        done = add(pr[j, 3], ar[0, j], ar[1, j])
-        gq_ref[:, j * qw : (j + 1) * qw] = done[:, :qw]
-        gk_ref[:, j * hd : (j + 1) * hd] = done[:, qw : qw + hd]
-        gv_ref[:, j * hd : (j + 1) * hd] = done[:, qw + hd :]
-
-    for j in range(chunks - 1):
-        final(j)
-
-    mine = block_rows(t)
-    for p in range(parts):
-        zcopy(1 - fwd, t, p, t).wait_recv()
-
-    @pl.when(m > 0)
-    def _():
-        for p in range(parts):
-            zcopy(fwd, t, p, t).wait_recv()
-
-    @pl.when(m == 0)
-    def _():
-        rb[fwd, t] = jnp.zeros((rows, width), BF16)
-
-    d_normed = dn[mine, :].astype(F32) + rb[0, t].astype(F32) + rb[1, t].astype(F32)
-    tokens2 = tok_ref[...].astype(F32)
-    inv2 = lax.rsqrt(jnp.mean(tokens2 * tokens2, -1, keepdims=True) + EPS)
-    unit = tokens2 * inv2
-    e = d_normed * gain_ref[...][None, :]
-    gtok_ref[...] = (inv2 * (e - unit * jnp.mean(e * unit, -1, keepdims=True))).astype(BF16)
-    final(chunks - 1)
-
     for j in range(chunks):
         wcopy(0, j, dp, px).wait_send()
         wcopy(1, j, dp, py).wait_send()
@@ -773,45 +793,97 @@
         wcopy(7, j, dp ^ 6, mate).wait_send()
         for i in range(n_chip):
             to_mate(j, i).wait_send()
-        for copy in (d_x, d_y, x_lo, x_hi, y_lo, y_hi):
+        for copy in (d_x, d_y):
             copy(j).wait_send()
     for h in range(2):
         for o in range(n_t - 1):
-            @pl.when((t - o >= 0) & (t + 1 < n_t))
+            split = o == 0 and h == 1
+
+            @pl.when((t - o >= 0) & (t + 1 < n_t - split))
             def _():
                 xcopy(0, o, h, t - o, t + 1).wait_send()
 
-            @pl.when((t + o < n_t) & (t > 0))
+            @pl.when((t + o < n_t) & (t > int(split)))
             def _():
                 xcopy(1, o, h, t + o, t - 1).wait_send()
 
+    @pl.when(m > 0)
+    def _():
+        for k in range(2):
+            qcopy(k, t, t - sign).wait_send()
+        for p in range(parts):
+            zcopy(fwd, mirror(n_t - 1), p, t + sign).wait_send()
+
+    @pl.when(m == 0)
+    def _():
+        for b in (n_t - 1, n_t - 2):
+            for p in range(parts):
+                zcopy(fwd, mirror(b), p, t + sign).wait_send()
+        rb[fwd, t] = jnp.zeros((rows, width), BF16)
+
+    for o in range(1, n_t):
+        p1(o).wait_send()
+    for j in range(chunks - 1):
+        final(j)
+    for copy in (x_lo, y_hi, x_hi, y_lo):
+        for j in range(chunks - 1):
+            copy(j).wait_send()
+    for o in range(1, n_dp):
+        p2r(o).wait_recv()
+    total = pb2[0]
+    for o in range(1, n_dp):
+        total = total + pb2[o]
+    gpre_ref[...] = total[0]
+    for o in range(1, n_dp):
+        p2(o).wait_send()
+
+    mine = block_rows(t)
+    tokens2 = tok_ref[...].astype(F32)
+    inv2 = lax.rsqrt(jnp.mean(tokens2 * tokens2, -1, keepdims=True) + EPS)
+    dots = jnp.zeros((rows, 1), F32)
+    held = []
     for p in range(parts):
-        for b in range(n_t - 1, 0, -1):
-            @pl.when(m < b)
-            def _():
-                zcopy(fwd, mirror(b), p, t + sign).wait_send()
+        cols = slice(p * tile, (p + 1) * tile)
+        zcopy(1 - fwd, t, p, t).wait_recv()
 
         @pl.when(m > 0)
         def _():
+            zcopy(fwd, t, p, t).wait_recv()
+
+        d_normed = (
+            dn[mine, cols].astype(F32) + rb[0, t, :, cols].astype(F32) + rb[1, t, :, cols].astype(F32)
+        )
+        unit = tok_ref[:, cols].astype(F32) * inv2
+        e = d_normed * gain_ref[cols][None, :]
+        dots = dots + jnp.sum(e * unit, -1, keepdims=True)
+        held.append((cols, unit, e))
+    mean = dots / width
+    for cols, unit, e in held:
+        gtok_ref[:, cols] = (inv2 * (e - unit * mean)).astype(BF16)
+    final(chunks - 1)
+
+    for copy in (x_lo, y_hi, x_hi, y_lo):
+        copy(chunks - 1).wait_send()
+    for p in range(parts):
+
+        @pl.when(m == 0)
+        def _():
+            zcopy(fwd, mirror(1), p, t + sign).wait_send()
+
+        @pl.when(m > 0)
+        def _():
+            zcopy(fwd, mirror(n_t - 2), p, t + sign).wait_send()
             zcopy(1 - fwd, mirror(0), p, t - sign).wait_send()
 
-    for o in range(1, n_dp):
-        p1(o).wait_send()
-    for o in range(1, n_t):
-        p2(o).wait_send()
-
-
-def finish_kernel(att, gtok, gq, gk, gv, gpre, *refs):
-    outs, (bq, bk, bv), sems = refs[:6], refs[6:9], refs[9]
+
+def finish_kernel(*refs):
+    count = len(refs) // 2
+    sems = refs[-1]
     copies = [
-        pltpu.make_async_copy(src, outs[i], sems.at[i])
-        for src, i in ((att, 0), (gtok, 1), (bq, 2), (bk, 3), (bv, 4), (gpre, 5))
+        pltpu.make_async_copy(refs[i], refs[count + i], sems.at[i]) for i in range(count)
     ]
-    for i in (0, 1, 5):
-        copies[i].start()
-    for src, wide, i in ((gq, bq, 2), (gk, bk, 3), (gv, bv, 4)):
-        wide[...] = src[...].astype(F32)
-        copies[i].start()
+    for copy in copies:
+        copy.start()
     for copy in copies:
         copy.wait()
 
@@ -846,9 +918,9 @@
         out_shape=(
             pltpu.VMEM((block, chunks * qw), BF16),
             pltpu.VMEM((rows, width), BF16),
-            pltpu.VMEM((shard, chunks * qw), BF16),
-            pltpu.VMEM((shard, kw), BF16),
-            pltpu.VMEM((shard, kw), BF16),
+            pltpu.VMEM((shard, chunks * qw), F32),
+            pltpu.VMEM((shard, kw), F32),
+            pltpu.VMEM((shard, kw), F32),
             pltpu.VMEM((width,), F32),
         ),
         in_specs=[hbm] * 9,
@@ -872,12 +944,14 @@
             pltpu.VMEM((2, chunks, shard, cw), BF16),
             pltpu.VMEM((block, width), BF16),
             pltpu.VMEM((2, n_t, rows, width), BF16),
+            pltpu.VMEM((n_t, 1, width), F32),
             pltpu.VMEM((n_dp, 1, width), F32),
-            pltpu.VMEM((n_t, 1, width), F32),
             dma((8, chunks)),
             dma((8, chunks)),
             dma((2, n_t, 2)),
             dma((2, n_t, 2)),
+            dma((2,)),
+            dma((2,)),
             dma((chunks, n_chip)),
             dma((chunks, n_chip)),
             dma((6, chunks)),
@@ -890,7 +964,7 @@
             dma((6,)),
         ],
         compiler_params=pltpu.CompilerParams(
-            collective_id=0, has_side_effects=True, vmem_limit_bytes=58 * 1024 * 1024
+            collective_id=0, has_side_effects=True, vmem_limit_bytes=57 * 1024 * 1024
         ),
     )(tokens, pre_gain, w_query, key_weight, value_weight, cotangent, cosine, sine, mask)
     return pl.pallas_call(
@@ -906,9 +980,6 @@
         in_specs=[vmem] * 6,
         out_specs=(hbm,) * 6,
         scratch_shapes=[
-            pltpu.VMEM((shard, chunks * qw), F32),
-            pltpu.VMEM((shard, kw), F32),
-            pltpu.VMEM((shard, kw), F32),
             dma((6,)),
         ],
         compiler_params=pltpu.CompilerParams(vmem_limit_bytes=16 * 1024 * 1024),

time: 102 us -> 97.7 us (0.958)
  Pallas kernels: 101 us -> 96.8 us
    pallas_call x1, Pallas kernels: 98.7 us -> 94.8 us  [fused_per_device(): pl.pallas_call(functools.partial(whole_kernel, (n_dp, n_t, chunks, rep, H...]
where the time goes in v2:
time: 97.7 us; the launch traced here: 97.6 us
  Pallas kernels  96.8 us (99%)
    pallas_call x1, Pallas kernels, fused_per_device(): pl.pallas_call(functools.partial(whole_kernel, (n_dp, n_t, chunks, rep, H...  94.8 us
    pallas_call x1, Pallas kernels, fused_per_device(): pl.pallas_call(finish_kernel, out_shape=(jax.ShapeDtypeStruct((block, chu...  1.99 us

profile of v2, /device:TPU:0, one launch (start us, length us, event | category | flops | bytes accessed | tf_op | source)
XLA Modules:
  0.0 97.6 jit_solution(9406134086544259725)
XLA Ops:
  0.6 94.8 %shard_map.136 = (bf16[512,1024]{1,0:T(8,128)(2,1)S(1)}, bf16[128,2304]{1,0:T(8,128)(2,1)S(1)}, f32[288,1024]{1,0:T(8,128)S(1)}, f32[288,512]{1,0:T(8,128)S(1)},...) custom-call(bf16[128,2304]{1,0:T(8,128)(2,1)} %tok_hbm.1, f32[2304]{0:T(1024)} %gain_hbm.1, bf16[288,1024]{1,0:T(8,128)(2,1)} %wq_ref.1, ...), custom_call_target="tpu_custom_call" | custom-call | tf_op jit(solution)/shard_map/pallas_call | solution.py:916
  95.4 2.0 %shard_map.137 = (bf16[512,1024]{1,0:T(8,128)(2,1)}, bf16[128,2304]{1,0:T(8,128)(2,1)}, f32[288,1024]{1,0:T(8,128)}, f32[288,512]{1,0:T(8,128)}, f32[288,512]{1,0:T(8,128)}, /*index=5*/f32[2304]{0:T(1024)}) custom-call(bf16[512,1024]{1,0:T(8,128)(2,1)S(1)} %get-tuple-element.12.refs_0_, bf16[128,2304]{1,0:T(8,128)(2,1)S(1)} %get-tuple-element.13.refs_1_, ...), custom_call_target="tpu_custom_call" | custom-call | tf_op jit(solution)/shard_map/pallas_call | solution.py:970

commit v3 on v2

--- a/solution.py
+++ b/solution.py
@@ -190,6 +190,9 @@
 def swap_halves(values):
     half = values.shape[-1] // 2
     return jnp.concatenate([values[:, half:], values[:, :half]], -1)
+
+
+W_SLOT = (0, 1, 2, 2, 2, 3, 3, 2)
 
 
 def whole_kernel(
@@ -233,7 +236,6 @@
     wr,
     xs,
     xr,
-    qs,
     qr,
     ms,
     mr,
@@ -299,15 +301,19 @@
         here = pl.ds(pl.multiple_of(dp * shard, 16), shard)
         return (
             pltpu.make_async_copy(
-                wq_ref.at[:, j * qw : (j + 1) * qw], w.at[j, here, 0:qw], ls.at[0, j]
+                wq_ref.at[:, j * qw : (j + 1) * qw], w.at[j, here, 0:qw], ls.at[j]
             ),
             pltpu.make_async_copy(
-                wk_ref.at[:, j * hd : (j + 1) * hd], w.at[j, here, qw : qw + hd], ls.at[1, j]
+                wk_ref.at[:, j * hd : (j + 1) * hd], w.at[j, here, qw : qw + hd], ls.at[j]
             ),
             pltpu.make_async_copy(
-                wv_ref.at[:, j * hd : (j + 1) * hd], w.at[j, here, qw + hd : cw], ls.at[2, j]
+                wv_ref.at[:, j * hd : (j + 1) * hd], w.at[j, here, qw + hd : cw], ls.at[j]
             ),
         )
+
+    def own_wait(j):
+        here = pl.ds(pl.multiple_of(dp * shard, 16), shard)
+        pltpu.make_async_copy(wq_ref.at[:, 0:cw], w.at[j, here], ls.at[j]).wait()
 
     loads[0].start()
     loads[1].start()
@@ -334,7 +340,11 @@
 
     def wcopy(kind, j, origin, to, h=None):
         place = w.at[j, wrow(origin, h)]
-        return rdma(place, place, ws.at[kind, j], wr.at[kind, j], to, t)
+        return rdma(place, place, ws.at[j], wr.at[W_SLOT[kind], j], to, t)
+
+    def whole(count, j, slot):
+        place = w.at[j, 0 : count * shard]
+        return rdma(place, place, ws.at[j], wr.at[slot, j], mate, t)
 
     def offer(j):
         wcopy(0, j, dp, px).start()
@@ -345,22 +355,25 @@
     m = jnp.where(low, t, n_t - 1 - t)
     fwd = jnp.where(low, 0, 1)
     piece, quarter = rows // 2, rows // 4
+    mine_next = t + sign
 
     def xcopy(way, o, h, origin, to):
         place = x.at[pl.ds(pl.multiple_of(origin * rows + h * piece, piece), piece)]
-        return rdma(place, place, xs.at[way, o, h], xr.at[way, o, h], dp, to)
+        return rdma(place, place, xs.at[min(o, 1)], xr.at[way, o, h], dp, to)
+
+    def xpart(origin, count, k):
+        place = x.at[pl.ds(pl.multiple_of(origin * rows, rows), count)]
+        return rdma(place, place, xs.at[k], qr.at[0], dp, mine_next)
 
     def qcopy(k, origin, to):
         first = pl.multiple_of(origin * rows + piece + k * quarter, quarter)
         place = x.at[pl.ds(first, quarter)]
-        return rdma(place, place, qs.at[k], qr.at[k], dp, to)
-
-    for copy in own_copies(0):
-        copy.wait()
+        return rdma(place, place, xs.at[0], qr.at[0], dp, to)
+
+    own_wait(0)
     pl.semaphore_wait(barrier, 3 + jnp.where(m == 0, 1, 2))
     offer(0)
-    for copy in own_copies(1):
-        copy.wait()
+    own_wait(1)
     offer(1)
     loads[0].wait()
     loads[1].wait()
@@ -391,8 +404,7 @@
         qcopy(0, t, t - sign).start()
 
     for j in range(2, chunks):
-        for copy in own_copies(j):
-            copy.wait()
+        own_wait(j)
     for j in range(chunks):
         wcopy(2, j, dp, mate).start()
     for copy in loads[2:]:
@@ -435,21 +447,16 @@
     def xfinish():
         @pl.when(m == 0)
         def _():
-            for k in range(2):
-                qcopy(k, t + sign, t).wait_recv()
+            xpart(t + sign, piece, 0).wait_recv()
 
     def far(j):
-        wcopy(5, j, dp ^ 6, py, h=0).wait_recv()
-        wcopy(6, j, dp ^ 6, px, h=1).wait_recv()
+        whole(1, j, 3).wait_recv()
         wcopy(7, j, dp ^ 6, mate).start()
 
     def ready(j, relayed=False):
         if not relayed:
             far(j)
-        wcopy(2, j, mate, mate).wait_recv()
-        wcopy(3, j, dp ^ 3, mate).wait_recv()
-        wcopy(4, j, dp ^ 5, mate).wait_recv()
-        wcopy(7, j, dp ^ 7, mate).wait_recv()
+        whole(n_chip, j, 2).wait_recv()
 
     factor = query_scalar ** (-0.5)
 
@@ -525,7 +532,7 @@
         return rdma(
             dn.at[block_rows(b), span(p)],
             rb.at[way, b, :, span(p)],
-            zs.at[way, b, p],
+            zs.at[0],
             zr.at[way, b, p],
             dp,
             to,
@@ -534,7 +541,7 @@
     def outward(b, p):
         zcopy(fwd, mirror(b), p, t + sign).start()
 
-    def back(first, count, sent):
+    def back(first, count, sent=None):
         here = block_rows(first, count)
 
         def cols(p, c2):
@@ -547,9 +554,11 @@
                 )
             dn[here, span(p)] = total.astype(BF16)
 
-            @pl.when(m == 0)
-            def _():
-                outward(sent, p)
+            if sent is not None:
+
+                @pl.when(m == 0)
+                def _():
+                    outward(sent, p)
 
             return c2
 
@@ -576,10 +585,10 @@
     lo, hi = pl.ds(0, half), pl.ds(half, half)
 
     def to_mate(j, i):
-        return rdma(g.at[j, i, 0], pr.at[j, i], ms.at[j, i], mr.at[j, i], mate, t)
+        return rdma(g.at[j, i, 0], pr.at[j, i], ms.at[j], mr.at[j, i], mate, t)
 
     def gcopy(kind, j, src, dst, to):
-        return rdma(src, dst, gs.at[kind, j], gr.at[kind, j], to, t)
+        return rdma(src, dst, gs.at[j], gr.at[min(kind, 2), j], to, t)
 
     def d_x(j):
         return gcopy(0, j, pr.at[j, 0, lo], dr.at[j, lo], px)
@@ -650,6 +659,7 @@
 
     far_block = mirror(n_t - 1)
     rest = jnp.where(low, 0, 1)
+    near_pair = jnp.where(low, 0, n_t - 2)
 
     def pass_far(p):
         @pl.when(m > 0)
@@ -670,22 +680,21 @@
             outward(n_t - 2, p)
 
     def p1(o):
-        return rdma(pb1.at[t], pb1.at[t], ps.at[0, o], prs.at[0, o], dp, t ^ o)
+        return rdma(pb1.at[t], pb1.at[t], ps.at[0], prs.at[0], dp, t ^ o)
 
     def p2(o):
-        return rdma(pb2.at[dp], pb2.at[dp], ps.at[1, o], prs.at[1, o], dp ^ o, t)
-
-    def p1r(o):
-        return rdma(pb1.at[t ^ o], pb1.at[t ^ o], ps.at[0, o], prs.at[0, o], dp, t ^ o)
-
-    def p2r(o):
-        return rdma(pb2.at[dp ^ o], pb2.at[dp ^ o], ps.at[1, o], prs.at[1, o], dp ^ o, t)
+        return rdma(pb2.at[dp], pb2.at[dp], ps.at[1], prs.at[1], dp ^ o, t)
+
+    def p1_all():
+        place = pb1.at[0 : n_t - 1]
+        return rdma(place, place, ps.at[0], prs.at[0], dp, mine_next)
+
+    def p2_all():
+        place = pb2.at[0 : n_dp - 1]
+        return rdma(place, place, ps.at[1], prs.at[1], mate, t)
 
     def final(j):
-        x_lo(j).wait_recv()
-        y_hi(j).wait_recv()
-        y_lo(j).wait_recv()
-        x_hi(j).wait_recv()
+        gcopy(2, j, pr.at[j, 0:2], ar.at[:, j], px).wait_recv()
         done = pr[j, 3].astype(F32) + ar[0, j].astype(F32) + ar[1, j].astype(F32)
         gq_ref[:, j * qw : (j + 1) * qw] = done[:, :qw]
         gk_ref[:, j * hd : (j + 1) * hd] = done[:, qw : qw + hd]
@@ -703,45 +712,50 @@
     xrelay(2, 0)
     relay(2)
     flip_weights(0)
-    ready(1)
+    far(1)
     xrelay(2, 1)
     xlate()
+    ready(1, True)
     tiles((1, 0), (0, 2), (1, 2))
     flip_rows(2)
     relay(3)
     flip_weights(1)
-    far(2)
     xrelay(3, 0)
     xrelay(3, 1)
     tiles((0, 3), (1, 3))
+    far(2)
     flip_rows(3)
     ready(2, True)
-    flip_weights(2)
+    xfinish()
     far(3)
-    tiles((2, 3))
-    xfinish()
-    tiles((0, 1))
+    tiles((0, 1), (2, 3))
     flip_rows(1)
     product(0, 0, 1)
     ready(3, True)
     tiles((3, 3))
     on_chip_far(0)
+    flip_weights(2)
     flip_weights(3)
     back(far_block, 1, n_t - 1)
     gain_part(far_block, 1, True)
     product(0, 1, 3)
+    tiles((1, 1))
     on_chip_near(0)
-    tiles((1, 1))
+    pass_on(0)
     product(1, 0, 3)
-    pass_on(0)
+    pass_far(0)
     on_chip_far(1)
-    tiles((2, 0), (2, 1), (2, 2))
+    tiles((2, 2), (3, 2))
     on_chip_near(1)
-    pass_far(0)
-    tiles((3, 0), (3, 1), (3, 2))
+    back(mirror(n_t - 2), 1, n_t - 2)
+    pass_far(1)
+    tiles((2, 0), (2, 1))
     product(2, 0, 1)
-    back(rest, n_t - 1, n_t - 2)
+    tiles((3, 0), (3, 1))
     on_chip_far(2)
+    pass_far(2)
+    back(near_pair, 2)
+    pass_on(1)
     gain_part(rest, n_t - 1, False)
     pb1[t] = pb1[t] / gain_ref[...][None, :]
     for o in range(1, n_t):
@@ -752,26 +766,22 @@
         for p in range(parts):
             outward(1, p)
 
-    pass_on(1)
-    pass_far(1)
-    pass_far(2)
     product(2, 1, 3)
+    product(3, 0, 3)
     on_chip_near(2)
-    product(3, 0, 3)
     pass_inner(0)
     on_chip_far(3)
     product(0, 3, 4)
     product(1, 3, 4)
     on_chip_near(3)
+    pass_on(2)
     pass_inner(1)
     pass_next(0)
-    pass_on(2)
     product(2, 3, 4)
     product(3, 3, 4)
     pass_inner(2)
     pass_next(1)
-    for o in range(1, n_t):
-        p1r(o).wait_recv()
+    p1_all().wait_recv()
     total = pb1[0]
     for o in range(1, n_t):
         total = total + pb1[o]
@@ -783,59 +793,29 @@
         joined(j, 3)
     pass_on(3)
     for j in range(chunks):
-        wcopy(0, j, dp, px).wait_send()
-        wcopy(1, j, dp, py).wait_send()
-        wcopy(2, j, dp, mate).wait_send()
-        wcopy(3, j, px, mate).wait_send()
-        wcopy(4, j, py, mate).wait_send()
-        wcopy(5, j, px, py, h=0).wait_send()
-        wcopy(6, j, py, px, h=1).wait_send()
-        wcopy(7, j, dp ^ 6, mate).wait_send()
-        for i in range(n_chip):
-            to_mate(j, i).wait_send()
-        for copy in (d_x, d_y):
-            copy(j).wait_send()
-    for h in range(2):
-        for o in range(n_t - 1):
-            split = o == 0 and h == 1
-
-            @pl.when((t - o >= 0) & (t + 1 < n_t - split))
-            def _():
-                xcopy(0, o, h, t - o, t + 1).wait_send()
-
-            @pl.when((t + o < n_t) & (t > int(split)))
-            def _():
-                xcopy(1, o, h, t + o, t - 1).wait_send()
+        whole(n_dp - 1, j, 2).wait_send()
+        rdma(g.at[j, :, 0], pr.at[j], ms.at[j], mr.at[j, 0], mate, t).wait_send()
+
+    @pl.when(m == 0)
+    def _():
+        xpart(0, rows, 0).wait_send()
+        rb[fwd, t] = jnp.zeros((rows, width), BF16)
 
     @pl.when(m > 0)
     def _():
-        for k in range(2):
-            qcopy(k, t, t - sign).wait_send()
-        for p in range(parts):
-            zcopy(fwd, mirror(n_t - 1), p, t + sign).wait_send()
-
-    @pl.when(m == 0)
-    def _():
-        for b in (n_t - 1, n_t - 2):
-            for p in range(parts):
-                zcopy(fwd, mirror(b), p, t + sign).wait_send()
-        rb[fwd, t] = jnp.zeros((rows, width), BF16)
-
-    for o in range(1, n_t):
-        p1(o).wait_send()
+        xpart(0, 2 * rows, 0).wait_send()
+        xpart(0, (n_t - 1) * rows, 1).wait_send()
+
+    p1_all().wait_send()
     for j in range(chunks - 1):
         final(j)
-    for copy in (x_lo, y_hi, x_hi, y_lo):
-        for j in range(chunks - 1):
-            copy(j).wait_send()
-    for o in range(1, n_dp):
-        p2r(o).wait_recv()
+        gcopy(2, j, pr.at[j, 0:3], pr.at[j, 0:3], px).wait_send()
+    p2_all().wait_recv()
     total = pb2[0]
     for o in range(1, n_dp):
         total = total + pb2[o]
     gpre_ref[...] = total[0]
-    for o in range(1, n_dp):
-        p2(o).wait_send()
+    p2_all().wait_send()
 
     mine = block_rows(t)
     tokens2 = tok_ref[...].astype(F32)
@@ -862,18 +842,9 @@
         gtok_ref[:, cols] = (inv2 * (e - unit * mean)).astype(BF16)
     final(chunks - 1)
 
-    for copy in (x_lo, y_hi, x_hi, y_lo):
-        copy(chunks - 1).wait_send()
-    for p in range(parts):
-
-        @pl.when(m == 0)
-        def _():
-            zcopy(fwd, mirror(1), p, t + sign).wait_send()
-
-        @pl.when(m > 0)
-        def _():
-            zcopy(fwd, mirror(n_t - 2), p, t + sign).wait_send()
-            zcopy(1 - fwd, mirror(0), p, t - sign).wait_send()
+    gcopy(2, chunks - 1, pr.at[chunks - 1, 0:3], pr.at[chunks - 1, 0:3], px).wait_send()
+    sent = dn.at[0 : (n_t - 1) * rows]
+    rdma(sent, sent, zs.at[0], zr.at[0, 0, 0], dp, mine_next).wait_send()
 
 
 def finish_kernel(*refs):
@@ -936,7 +907,7 @@
             pltpu.VMEM((width, block), BF16),
             pltpu.VMEM((chunks, width, cw), BF16),
             pltpu.VMEM((chunks, cw, width), BF16),
-            pltpu.VMEM((3, rows, cw), F32),
+            pltpu.VMEM((4, rows, cw), F32),
             pltpu.VMEM((chunks, block, cw), BF16),
             pltpu.VMEM((chunks, n_chip, 2, shard, cw), BF16),
             pltpu.VMEM((chunks, n_chip, shard, cw), BF16),
@@ -946,21 +917,20 @@
             pltpu.VMEM((2, n_t, rows, width), BF16),
             pltpu.VMEM((n_t, 1, width), F32),
             pltpu.VMEM((n_dp, 1, width), F32),
-            dma((8, chunks)),
-            dma((8, chunks)),
-            dma((2, n_t, 2)),
-            dma((2, n_t, 2)),
+            dma((chunks,)),
+            dma((4, chunks)),
+            dma((2,)),
+            dma((2, n_t - 1, 2)),
+            dma((1,)),
+            dma((chunks,)),
+            dma((chunks, n_chip)),
+            dma((chunks,)),
+            dma((3, chunks)),
+            dma((1,)),
+            dma((2, n_t, parts)),
             dma((2,)),
             dma((2,)),
-            dma((chunks, n_chip)),
-            dma((chunks, n_chip)),
-            dma((6, chunks)),
-            dma((6, chunks)),
-            dma((2, n_t, parts)),
-            dma((2, n_t, parts)),
-            dma((2, n_dp)),
-            dma((2, n_dp)),
-            dma((3, chunks)),
+            dma((chunks,)),
             dma((6,)),
         ],
         compiler_params=pltpu.CompilerParams(

time: 97.7 us -> 95.7 us (0.980)
  Pallas kernels: 96.8 us -> 94.8 us
    pallas_call x1, Pallas kernels: 94.8 us -> 92.8 us  [fused_per_device(): pl.pallas_call(functools.partial(whole_kernel, (n_dp, n_t, chunks, rep, H...]
where the time goes in v3:
time: 95.7 us; the launch traced here: 95.6 us
  Pallas kernels  94.8 us (99%)
    pallas_call x1, Pallas kernels, fused_per_device(): pl.pallas_call(functools.partial(whole_kernel, (n_dp, n_t, chunks, rep, H...  92.8 us
    pallas_call x1, Pallas kernels, fused_per_device(): pl.pallas_call(finish_kernel, out_shape=(jax.ShapeDtypeStruct((block, chu...  1.99 us

profile of v3, /device:TPU:0, one launch (start us, length us, event | category | flops | bytes accessed | tf_op | source)
XLA Modules:
  0.0 95.6 jit_solution(6549405128986584982)
XLA Ops:
  0.6 92.8 %shard_map.136 = (bf16[512,1024]{1,0:T(8,128)(2,1)S(1)}, bf16[128,2304]{1,0:T(8,128)(2,1)S(1)}, f32[288,1024]{1,0:T(8,128)S(1)}, f32[288,512]{1,0:T(8,128)S(1)},...) custom-call(bf16[128,2304]{1,0:T(8,128)(2,1)} %tok_hbm.1, f32[2304]{0:T(1024)} %gain_hbm.1, bf16[288,1024]{1,0:T(8,128)(2,1)} %wq_ref.1, ...), custom_call_target="tpu_custom_call" | custom-call | tf_op jit(solution)/shard_map/pallas_call | solution.py:887
  93.4 2.0 %shard_map.137 = (bf16[512,1024]{1,0:T(8,128)(2,1)}, bf16[128,2304]{1,0:T(8,128)(2,1)}, f32[288,1024]{1,0:T(8,128)}, f32[288,512]{1,0:T(8,128)}, f32[288,512]{1,0:T(8,128)}, /*index=5*/f32[2304]{0:T(1024)}) custom-call(bf16[512,1024]{1,0:T(8,128)(2,1)S(1)} %get-tuple-element.12.refs_0_, bf16[128,2304]{1,0:T(8,128)(2,1)S(1)} %get-tuple-element.13.refs_1_, ...), custom_call_target="tpu_custom_call" | custom-call | tf_op jit(solution)/shard_map/pallas_call | solution.py:940

commit v4 on v3

--- a/solution.py
+++ b/solution.py
@@ -533,7 +533,7 @@
             dn.at[block_rows(b), span(p)],
             rb.at[way, b, :, span(p)],
             zs.at[0],
-            zr.at[way, b, p],
+            zr.at[way, b - 1 + way, p],
             dp,
             to,
         )
@@ -541,17 +541,19 @@
     def outward(b, p):
         zcopy(fwd, mirror(b), p, t + sign).start()
 
-    def back(first, count, sent=None):
+    def back(first, count, sent=None, begin=0, end=parts, flipped=chunks):
         here = block_rows(first, count)
 
         def cols(p, c2):
-            total = lax.dot_general(
-                dproj[0, here, :], wt[0, :, span(p)], NN, preferred_element_type=F32
-            )
-            for j in range(1, chunks):
+            total = jnp.zeros((count * rows, tile), F32)
+            for j in range(flipped):
                 total += lax.dot_general(
                     dproj[j, here, :], wt[j, :, span(p)], NN, preferred_element_type=F32
                 )
+            for j in range(flipped, chunks):
+                total += lax.dot_general(
+                    dproj[j, here, :], w[j, span(p), :], NT, preferred_element_type=F32
+                )
             dn[here, span(p)] = total.astype(BF16)
 
             if sent is not None:
@@ -562,7 +564,7 @@
 
             return c2
 
-        lax.fori_loop(0, parts, cols, 0)
+        lax.fori_loop(begin, end, cols, 0)
 
     strip = 64
 
@@ -585,10 +587,10 @@
     lo, hi = pl.ds(0, half), pl.ds(half, half)
 
     def to_mate(j, i):
-        return rdma(g.at[j, i, 0], pr.at[j, i], ms.at[j], mr.at[j, i], mate, t)
+        return rdma(g.at[j, i, 0], pr.at[j, i], ms.at[j], mr.at[j, (i + 1) // 2], mate, t)
 
     def gcopy(kind, j, src, dst, to):
-        return rdma(src, dst, gs.at[j], gr.at[min(kind, 2), j], to, t)
+        return rdma(src, dst, gs.at[j], gr.at[min(kind // 2, 1), j], to, t)
 
     def d_x(j):
         return gcopy(0, j, pr.at[j, 0, lo], dr.at[j, lo], px)
@@ -638,16 +640,17 @@
         d_y(j).start()
 
     def on_chip_near(j):
-        joined(j, 1)
+        pair = pr.at[j, 1:3]
+        rdma(pair, pair, ms.at[j], mr.at[j, 1], mate, t).wait_recv()
+        pr[j, 1] = add(g[j, 1, 1], pr[j, 1])
         y_hi(j).start()
-        joined(j, 2)
+        pr[j, 2] = add(g[j, 2, 1], pr[j, 2])
         x_lo(j).start()
 
     def pass_on(j):
-        d_x(j).wait_recv()
+        gcopy(0, j, pr.at[j, 0], dr.at[j], px).wait_recv()
         pr[j, 1, lo] = add(pr[j, 1, lo], dr[j, lo])
         y_lo(j).start()
-        d_y(j).wait_recv()
         pr[j, 2, hi] = add(pr[j, 2, hi], dr[j, hi])
         x_hi(j).start()
 
@@ -722,8 +725,8 @@
     flip_weights(1)
     xrelay(3, 0)
     xrelay(3, 1)
+    far(2)
     tiles((0, 3), (1, 3))
-    far(2)
     flip_rows(3)
     ready(2, True)
     xfinish()
@@ -734,28 +737,33 @@
     ready(3, True)
     tiles((3, 3))
     on_chip_far(0)
-    flip_weights(2)
-    flip_weights(3)
-    back(far_block, 1, n_t - 1)
+    back(far_block, 1, n_t - 1, 0, 1, 2)
+    product(0, 1, 3)
+    back(far_block, 1, n_t - 1, 1, 2, 2)
+    on_chip_near(0)
+    back(far_block, 1, n_t - 1, 2, parts, 2)
     gain_part(far_block, 1, True)
-    product(0, 1, 3)
     tiles((1, 1))
-    on_chip_near(0)
     pass_on(0)
     product(1, 0, 3)
     pass_far(0)
+    flip_weights(2)
     on_chip_far(1)
+    flip_weights(3)
     tiles((2, 2), (3, 2))
     on_chip_near(1)
-    back(mirror(n_t - 2), 1, n_t - 2)
+    back(mirror(n_t - 2), 1, n_t - 2, 0, parts - 1)
+    back(mirror(n_t - 2), 1, None, parts - 1, parts)
     pass_far(1)
     tiles((2, 0), (2, 1))
     product(2, 0, 1)
+    pass_on(1)
     tiles((3, 0), (3, 1))
     on_chip_far(2)
     pass_far(2)
+    product(2, 1, 3)
     back(near_pair, 2)
-    pass_on(1)
+    on_chip_near(2)
     gain_part(rest, n_t - 1, False)
     pb1[t] = pb1[t] / gain_ref[...][None, :]
     for o in range(1, n_t):
@@ -763,12 +771,11 @@
 
     @pl.when(m == 0)
     def _():
+        outward(n_t - 2, parts - 1)
         for p in range(parts):
             outward(1, p)
 
-    product(2, 1, 3)
     product(3, 0, 3)
-    on_chip_near(2)
     pass_inner(0)
     on_chip_far(3)
     product(0, 3, 4)
@@ -810,12 +817,6 @@
     for j in range(chunks - 1):
         final(j)
         gcopy(2, j, pr.at[j, 0:3], pr.at[j, 0:3], px).wait_send()
-    p2_all().wait_recv()
-    total = pb2[0]
-    for o in range(1, n_dp):
-        total = total + pb2[o]
-    gpre_ref[...] = total[0]
-    p2_all().wait_send()
 
     mine = block_rows(t)
     tokens2 = tok_ref[...].astype(F32)
@@ -840,8 +841,14 @@
     mean = dots / width
     for cols, unit, e in held:
         gtok_ref[:, cols] = (inv2 * (e - unit * mean)).astype(BF16)
+    p2_all().wait_recv()
+    total = pb2[0]
+    for o in range(1, n_dp):
+        total = total + pb2[o]
+    gpre_ref[...] = total[0]
     final(chunks - 1)
 
+    p2_all().wait_send()
     gcopy(2, chunks - 1, pr.at[chunks - 1, 0:3], pr.at[chunks - 1, 0:3], px).wait_send()
     sent = dn.at[0 : (n_t - 1) * rows]
     rdma(sent, sent, zs.at[0], zr.at[0, 0, 0], dp, mine_next).wait_send()
@@ -923,11 +930,11 @@
             dma((2, n_t - 1, 2)),
             dma((1,)),
             dma((chunks,)),
-            dma((chunks, n_chip)),
+            dma((chunks, 3)),
             dma((chunks,)),
-            dma((3, chunks)),
+            dma((2, chunks)),
             dma((1,)),
-            dma((2, n_t, parts)),
+            dma((2, n_t - 1, parts)),
             dma((2,)),
             dma((2,)),
             dma((chunks,)),

time: 95.7 us -> 92.9 us (0.971)
  Pallas kernels: 94.8 us -> 92 us
    pallas_call x1, Pallas kernels: 92.8 us -> 90 us  [fused_per_device(): pl.pallas_call(functools.partial(whole_kernel, (n_dp, n_t, chunks, rep, H...]
where the time goes in v4:
time: 92.9 us; the launch traced here: 92.8 us
  Pallas kernels  92 us (99%)
    pallas_call x1, Pallas kernels, fused_per_device(): pl.pallas_call(functools.partial(whole_kernel, (n_dp, n_t, chunks, rep, H...  90 us
    pallas_call x1, Pallas kernels, fused_per_device(): pl.pallas_call(finish_kernel, out_shape=(jax.ShapeDtypeStruct((block, chu...  1.99 us

profile of v4, /device:TPU:0, one launch (start us, length us, event | category | flops | bytes accessed | tf_op | source)
XLA Modules:
  0.0 92.8 jit_solution(15842933060861249960)
XLA Ops:
  0.6 90.0 %shard_map.136 = (bf16[512,1024]{1,0:T(8,128)(2,1)S(1)}, bf16[128,2304]{1,0:T(8,128)(2,1)S(1)}, f32[288,1024]{1,0:T(8,128)S(1)}, f32[288,512]{1,0:T(8,128)S(1)},...) custom-call(bf16[128,2304]{1,0:T(8,128)(2,1)} %tok_hbm.1, f32[2304]{0:T(1024)} %gain_hbm.1, bf16[288,1024]{1,0:T(8,128)(2,1)} %wq_ref.1, ...), custom_call_target="tpu_custom_call" | custom-call | tf_op jit(solution)/shard_map/pallas_call | solution.py:894
  90.6 2.0 %shard_map.137 = (bf16[512,1024]{1,0:T(8,128)(2,1)}, bf16[128,2304]{1,0:T(8,128)(2,1)}, f32[288,1024]{1,0:T(8,128)}, f32[288,512]{1,0:T(8,128)}, f32[288,512]{1,0:T(8,128)}, /*index=5*/f32[2304]{0:T(1024)}) custom-call(bf16[512,1024]{1,0:T(8,128)(2,1)S(1)} %get-tuple-element.12.refs_0_, bf16[128,2304]{1,0:T(8,128)(2,1)S(1)} %get-tuple-element.13.refs_1_, ...), custom_call_target="tpu_custom_call" | custom-call | tf_op jit(solution)/shard_map/pallas_call | solution.py:947
